TPU v7x, 32 devices: a whole 2x2x4 slice. The times are simulated.
32 devices in a mesh: space: 16 (over z, y, core), tensor: 2 (over x).
Axes of the slice: x: 2, y: 2, z: 4, core: 2. Of those that a mesh axis runs over, the one named last changes fastest.
Arguments:
- tokens: bfloat16 [14336, 1024], P('space', 'tensor'), may hold values from -6 to 6
- first_weight: bfloat16 [1024, 1024], P(None, 'tensor'), may hold values from -0.1875 to 0.1875
- second_weight: bfloat16 [1024, 1024], P(None, 'tensor'), may hold values from -0.1875 to 0.1875
- head_weight: bfloat16 [352, 1024], P('tensor'), may hold values from -0.1875 to 0.1875
- targets: float32 [352, 14336], P('tensor', 'space'), may hold values from -6 to 6
- land_mask: int32 [4, 14336], P(None, 'space'), may hold values from 0 to 1, as said below
- variable_kind: int32 [88], P('tensor'), may hold values from 0 to 2
- loss_scale: float32 [], replicated, may hold values from 630784 to 5046272
Outputs:
- loss: float32 [], replicated
- token_grad: float32 [14336, 1024], P('space', 'tensor')
- first_grad: float32 [1024, 1024], P('space', 'tensor')
- second_grad: float32 [1024, 1024], P('space', 'tensor')
- head_grad: float32 [352, 1024], P('tensor', 'space')
Inputs may be any that keep to these rules, and one draw needn't show every extreme that they name: `land_mask`: every aligned group of 8 entries along the last dimension holds at least one 1 and one 0. `variable_kind`: 0 scores a variable on all cells, 1 on land cells, 2 on ocean cells.
All inputs are finite; a program needn't handle non-finite values.
Results may differ from a plain program's by a relative error of at most 0.0056.
Values may be sent and summed in bfloat16 or wider, within the bound.
A program may use at most 64 MiB of HBM per device.

v0:
```python
import math

import jax
import jax.numpy as jnp
from jax import lax
from jax.sharding import PartitionSpec as P

V = 88
PP = 4
PROW_DEV = 4
LONP = 224


def slope(z):
    cdf = 0.5 * (1.0 + lax.erf(z / math.sqrt(2.0)))
    return cdf + z * jnp.exp(-0.5 * z * z) / math.sqrt(2.0 * math.pi)


def column_folder(weights, piece):
    return lax.dot_general(
        piece, weights, (((1,), (1,)), ((), ())), preferred_element_type=jnp.float32
    )


def row_folder(weights, piece):
    return lax.dot_general(
        piece, weights, (((0,), (0,)), ((), ())), preferred_element_type=jnp.float32
    )


def per_device(
    tokens, first_weight, second_weight, head_weight, targets, land_mask, variable_kind, loss_scale
):
    count = tokens.shape[0]
    width = first_weight.shape[1]
    kinds = head_weight.shape[0] // PP
    rows_first, rows_second = (
        lax.all_to_all(first_weight, "tensor", split_axis=0, concat_axis=1, tiled=True),
        lax.all_to_all(second_weight, "tensor", split_axis=0, concat_axis=1, tiled=True),
    )
    head_cols = lax.all_to_all(head_weight, "tensor", split_axis=1, concat_axis=0, tiled=True)
    position = lax.axis_index("space") * count + jnp.arange(count, dtype=jnp.int32)
    cell = jnp.arange(PP, dtype=jnp.int32)
    lat_row = 2 * (position // LONP)[None, :] + (cell // 2)[:, None]
    nlat = 2 * PROW_DEV * lax.axis_size("space")
    cell_weight = jnp.cos(math.pi / 2.0 * (lat_row.astype(jnp.float32) + 0.5) / nlat)
    land = land_mask.astype(jnp.float32)
    kind = variable_kind[:, None, None]
    valid = jnp.where(kind == 0, 1.0, jnp.where(kind == 1, land[None], 1.0 - land[None]))
    masked = cell_weight[None] * valid
    local_weight = jnp.sum(masked, axis=(1, 2))
    weight_sum = lax.psum(local_weight, "space")
    full_in = lax.all_gather(tokens, "tensor", axis=1, tiled=True)
    pre_one = jnp.dot(full_in, first_weight, preferred_element_type=jnp.float32)
    hidden_one = jax.nn.gelu(pre_one, approximate=False).astype(jnp.bfloat16)
    full_one = lax.all_gather(hidden_one, "tensor", axis=1, tiled=True)
    pre_two = jnp.dot(full_one, second_weight, preferred_element_type=jnp.float32)
    hidden_two = jax.nn.gelu(pre_two, approximate=False).astype(jnp.bfloat16)
    full_two = lax.all_gather(hidden_two, "tensor", axis=1, tiled=True)
    predicted = lax.dot_general(
        head_weight, full_two, (((1,), (1,)), ((), ())), preferred_element_type=jnp.float32
    )
    error = predicted.reshape(kinds, PP, count) - targets.reshape(kinds, PP, count)
    local_error = jnp.sum(masked * error * error, axis=(1, 2))
    error_sum = lax.psum(local_error, "space")
    root = jnp.sqrt(error_sum / weight_sum + 1e-06)
    loss = lax.psum(jnp.sum(root), "tensor") / V
    coef = loss_scale / (V * root * weight_sum)
    grad_pred = (
        (coef[:, None, None] * masked * error).reshape(kinds * PP, count).astype(jnp.bfloat16)
    )
    back_two = row_folder(head_cols, lax.all_gather(grad_pred, "tensor", axis=0, tiled=True))
    head_term = jnp.dot(grad_pred, full_two, preferred_element_type=jnp.float32)
    head_grad = lax.psum_scatter(head_term, "space", scatter_dimension=1, tiled=True)
    grad_two = (back_two * slope(pre_two)).astype(jnp.bfloat16)
    back_one = column_folder(rows_second, lax.all_gather(grad_two, "tensor", axis=1, tiled=True))
    grad_one = (back_one * slope(pre_one)).astype(jnp.bfloat16)
    joined = lax.psum_scatter(
        jnp.concatenate(
            [
                lax.dot_general(
                    full_one, grad_two, (((0,), (0,)), ((), ())), preferred_element_type=jnp.float32
                ),
                lax.dot_general(
                    full_in, grad_one, (((0,), (0,)), ((), ())), preferred_element_type=jnp.float32
                ),
            ],
            axis=1,
        ),
        "space",
        scatter_dimension=0,
        tiled=True,
    )
    second_grad = joined[:, :width]
    first_grad = joined[:, width:]
    token_grad = column_folder(rows_first, lax.all_gather(grad_one, "tensor", axis=1, tiled=True))
    return (loss, token_grad, first_grad, second_grad, head_grad)


def solution(mesh):
    return jax.shard_map(
        per_device,
        mesh=mesh,
        in_specs=(
            P("space", "tensor"),
            P(None, "tensor"),
            P(None, "tensor"),
            P("tensor", None),
            P("tensor", "space"),
            P(None, "space"),
            P("tensor"),
            P(),
        ),
        out_specs=(
            P(),
            P("space", "tensor"),
            P("space", "tensor"),
            P("space", "tensor"),
            P("tensor", "space"),
        ),
        check_vma=False,
    )
```

profile of v0, /device:TPU:0, one launch (start us, length us, event | category | flops | bytes accessed | tf_op | source)
XLA Modules:
  0.0 390.4 jit_solution(11387166332372937541)
XLA Ops:
  8.0 34.5 %all-gather.6.cloned.1.call-done = bf16[896,1024]{1,0:T(8,128)(2,1)} async-done(((bf16[896,512]{1,0:T(8,128)(2,1)}), bf16[896,1024]{1,0:T(8,128)(2,1)}) %all-gather.6.cloned.1.call-update) | async-done | bytes 1835024 | tf_op jit(solution)/shard_map/all_gather | solution.py:53
  42.4 8.0 %fusion.2 = (bf16[896,512]{1,0:T(8,128)(2,1)}, f32[896,512]{1,0:T(8,128)}) fusion(bf16[896,1024]{1,0:T(8,128)(2,1)} %all-gather.6.cloned.1.call-done, bf16[1024,512]{1,0:T(8,128)(2,1)} %param.9), kind=kOutput, calls=%fused_computation.7 | convolution fusion | flops 969342976 | bytes 5636096 | tf_op jit(solution)/shard_map/dot_general | solution.py:54
  50.5 30.2 %all-gather.8.cloned.1.call-done = bf16[896,1024]{1,0:T(8,128)(2,1)} async-done(((bf16[896,512]{1,0:T(8,128)(2,1)}), bf16[896,1024]{1,0:T(8,128)(2,1)}) %all-gather.8.cloned.1.call-update) | async-done | bytes 1835024 | tf_op jit(solution)/shard_map/all_gather | solution.py:56
  80.7 7.5 %fusion.5 = (bf16[896,512]{1,0:T(8,128)(2,1)}, f32[896,512]{1,0:T(8,128)}) fusion(bf16[896,1024]{1,0:T(8,128)(2,1)} %all-gather.8.cloned.1.call-done, bf16[1024,512]{1,0:T(8,128)(2,1)S(1)} %copy-done.4), kind=kOutput, calls=%fused_computation.10 | convolution fusion | flops 969342976 | bytes 5636096 | tf_op jit(solution)/shard_map/dot_general | solution.py:57
  89.0 4.2 %all-to-all-start = ((bf16[176,2,512]{2,0,1:T(8,128)(2,1)}), bf16[176,2,512]{2,0,1:T(8,128)(2,1)}, u32[]{:S(2)}, u32[]{:S(2)}) async-start(bf16[176,2,512]{2,0,1:T(8,128)(2,1)} %bitcast.37), calls=%async_computation | async-start | bytes 720896 | tf_op jit(solution)/shard_map/all_to_all | solution.py:41
  96.3 23.1 %all-gather.10.cloned.1.call-done = bf16[896,1024]{1,0:T(8,128)(2,1)} async-done(((bf16[896,512]{1,0:T(8,128)(2,1)}), bf16[896,1024]{1,0:T(8,128)(2,1)}) %all-gather.10.cloned.1.call-update) | async-done | bytes 1835024 | tf_op jit(solution)/shard_map/all_gather | solution.py:59
  119.4 2.6 fusion.33
  122.2 33.2 %all-reduce = (f32[44]{0:T(128)S(1)}, f32[44]{0:T(128)S(1)}) all-reduce(f32[44]{0:T(128)S(1)} %reduce_sum.36, f32[44]{0:T(128)S(1)} %multiply_reduce_fusion), channel_id=1, replica_groups=mesh['space'=16,'tensor'=2] {'space'}, use_global_device_ids=true, to_apply=%region_2.3 | all-reduce | flops 88 | bytes 704 | tf_op jit(solution)/shard_map/psum | solution.py:65
  155.8 7.6 %all_gather.21 = bf16[352,896]{1,0:T(8,128)(2,1)S(1)} all-gather(bf16[176,896]{1,0:T(8,128)(2,1)S(1)} %multiply_convert_fusion), channel_id=1, replica_groups=mesh['space'=16,'tensor'=2] {'tensor'}, dimensions={0}, use_global_device_ids=true | all-gather | bytes 946176 | tf_op jit(solution)/shard_map/all_gather | solution.py:72
  163.4 3.7 fusion.11
  167.2 22.7 %all_to_all.57 = bf16[2,512,512]{2,1,0:T(8,128)(2,1)S(1)} all-to-all(bf16[2,512,512]{2,1,0:T(8,128)(2,1)S(1)} %bitcast.41), channel_id=1, replica_groups=mesh['space'=16,'tensor'=2] {'tensor'}, dimensions={0} | all-to-all | bytes 2097152 | tf_op jit(solution)/shard_map/all_to_all | solution.py:39
  190.4 8.6 %all-gather.12.cloned.1.call-done = bf16[896,1024]{1,0:T(8,128)(2,1)} async-done(((bf16[896,512]{1,0:T(8,128)(2,1)}), bf16[896,1024]{1,0:T(8,128)(2,1)}) %all-gather.12.cloned.1.call-update) | async-done | bytes 1835024 | tf_op jit(solution)/shard_map/all_gather | solution.py:76
  199.0 4.6 %fusion.17 = bf16[896,512]{1,0:T(8,128)(2,1)} fusion(f32[896,512]{1,0:T(8,128)} %get-tuple-element.36, bf16[896,1024]{1,0:T(8,128)(2,1)} %all-gather.12.cloned.1.call-done, bf16[512,1024]{0,1:T(8,128)(2,1)S(1)} %bitcast.44), kind=kOutput, calls=%fused_computation.22 | convolution fusion | flops 944111616 | bytes 5636096 | tf_op jit(solution)/shard_map/dot_general | solution.py:20
  203.7 3.2 fusion.38
  208.1 2.5 pad_maximum_fusion
  210.6 5.5 %copy.27 = f32[1024,1024]{1,0:T(8,128)} copy(f32[1024,1024]{0,1:T(8,128)} %pad_maximum_fusion) | data formatting | bytes 8388608
  216.2 3.7 all-to-all-start.2
  220.0 1.9 fusion.39
  222.5 22.4 %all-to-all-done.2 = bf16[2,512,512]{2,1,0:T(8,128)(2,1)S(1)} async-done(((bf16[2,512,512]{2,1,0:T(8,128)(2,1)}), bf16[2,512,512]{2,1,0:T(8,128)(2,1)S(1)}, u32[]{:S(2)}, u32[]{:S(2)}) %all-to-all-start.2) | async-done | bytes 1048608 | tf_op jit(solution)/shard_map/all_to_all | solution.py:38
  245.4 5.6 %psum.23 = f32[]{:T(128)} all-reduce(f32[]{:T(128)} %reduce_sum.38), channel_id=1, replica_groups=mesh['space'=16,'tensor'=2] {'tensor'}, use_global_device_ids=true, to_apply=%region_6.7 | all-reduce | flops 1 | bytes 8 | tf_op jit(solution)/shard_map/psum | solution.py:67
  251.7 3.9 fusion.37
  255.5 66.0 %reduce-scatter.7.cloned.1.call-done = f32[64,1024]{1,0:T(8,128)} async-done(((f32[1024,1024]{1,0:T(8,128)}), f32[64,1024]{1,0:T(8,128)}) %reduce-scatter.7.cloned.1.call-update) | async-done | bytes 262160
  321.5 1.7 fusion.36
  323.2 59.2 %reduce-scatter.5.cloned.1.call-done = f32[176,64]{0,1:T(8,128)} async-done(((f32[176,1024]{0,1:T(8,128)}), f32[176,64]{0,1:T(8,128)}) %reduce-scatter.5.cloned.1.call-update) | async-done | bytes 45072 | tf_op jit(solution)/shard_map/reduce_scatter | solution.py:74
  (59 shorter events, 7.7 us)
Async XLA Ops:
  7.2 35.2 %all-gather.6.cloned.1.call-start = ((), (), s32[]{:S(2)}) async-start(), calls=%async_computation.5 | async-start | bytes 2752512 | tf_op jit(solution)/shard_map/all_gather | solution.py:53
  7.9 72.8 %copy-start.4 = (bf16[1024,512]{1,0:T(8,128)(2,1)S(1)}, bf16[1024,512]{1,0:T(8,128)(2,1)}, u32[]{:S(2)}) copy-start(bf16[1024,512]{1,0:T(8,128)(2,1)} %param.10) | copy-start | bytes 3145732
  7.9 72.8 %all-gather.8.cloned.1.call-start = ((), (), s32[]{:S(2)}) async-start(), calls=%async_computation.6 | async-start | bytes 2752512 | tf_op jit(solution)/shard_map/all_gather | solution.py:56
  50.4 37.8 %copy-start.3 = (bf16[176,1024]{1,0:T(8,128)(2,1)S(1)}, bf16[176,1024]{1,0:T(8,128)(2,1)}, u32[]{:S(2)}) copy-start(bf16[176,1024]{1,0:T(8,128)(2,1)} %param.11) | copy-start | bytes 1081348
  50.4 69.0 %all-gather.10.cloned.1.call-start = ((), (), s32[]{:S(2)}) async-start(), calls=%async_computation.7 | async-start | bytes 2752512 | tf_op jit(solution)/shard_map/all_gather | solution.py:59
  88.2 5.0 %copy-start.6 = (s32[4,896]{1,0:T(4,128)S(1)}, s32[4,896]{1,0:T(4,128)}, u32[]{:S(2)}) copy-start(s32[4,896]{1,0:T(4,128)} %param.13) | copy-start | bytes 43012
  89.0 74.4 %all-to-all-start = ((bf16[176,2,512]{2,0,1:T(8,128)(2,1)}), bf16[176,2,512]{2,0,1:T(8,128)(2,1)}, u32[]{:S(2)}, u32[]{:S(2)}) async-start(bf16[176,2,512]{2,0,1:T(8,128)(2,1)} %bitcast.37), calls=%async_computation | async-start | bytes 720896 | tf_op jit(solution)/shard_map/all_to_all | solution.py:41
  93.2 105.8 %all-gather.12.cloned.1.call-start = ((), (), s32[]{:S(2)}) async-start(), calls=%async_computation.8 | async-start | bytes 2752512 | tf_op jit(solution)/shard_map/all_gather | solution.py:76
  93.8 0.7 copy-start.7
  163.4 3.8 copy-start.5
  167.2 84.5 %all-gather.14.cloned.1.call-start = ((), (), s32[]{:S(2)}) async-start(), calls=%async_computation.9 | async-start | bytes 2752512 | tf_op jit(solution)/shard_map/all_gather | solution.py:96
  203.6 3.2 copy-start.1
  203.6 3.2 copy-start.2
  203.6 117.9 %reduce-scatter.7.cloned.1.call-start = ((), (), s32[]{:S(2)}) async-start(), calls=%async_computation.11 | async-start | bytes 4456448
  216.2 3.8 copy-start
  216.2 28.7 %all-to-all-start.2 = ((bf16[2,512,512]{2,1,0:T(8,128)(2,1)}), bf16[2,512,512]{2,1,0:T(8,128)(2,1)S(1)}, u32[]{:S(2)}, u32[]{:S(2)}) async-start(bf16[2,512,512]{2,1,0:T(8,128)(2,1)} %bitcast.42), calls=%async_computation.2 | async-start | bytes 2097152 | tf_op jit(solution)/shard_map/all_to_all | solution.py:38
  219.9 162.5 %reduce-scatter.5.cloned.1.call-start = ((), (), s32[]{:S(2)}) async-start(), calls=%async_computation.10 | async-start | bytes 1114112 | tf_op jit(solution)/shard_map/reduce_scatter | solution.py:74
Sparse Core Ops, SparseCore 0:
  9.5 32.8 all-gather.5
  50.5 30.1 all-gather.7
  88.3 31.0 all-gather.9
  167.3 31.6 all-gather.11
  203.7 40.9 all-gather.13
  248.5 72.9 reduce-scatter.6
  325.7 56.6 reduce-scatter.4
where the time goes:
time: 391 us; the launch traced here: 390 us
  waiting for transfers between devices  245 us (63%)
  blocking collectives  69.1 us (18%)
  matrix products  36.5 us (9%)
  between operations  16.8 us (4%)
  local copies, waits for them, and re-layouts  10.7 us (3%)
  starting transfers between devices  8.16 us (2%)
  other arithmetic  4.37 us (1%)
    unnamed x8, waiting for transfers between devices  66.7 us
    reduce_scatter x1, waiting for transfers between devices, per_device(): lax.psum_scatter(head_term, 'space', scatter_dimension=1, tiled=True)  59.2 us
    all_gather x1, waiting for transfers between devices, per_device(): full_in = lax.all_gather(tokens, 'tensor', axis=1, tiled=True)  34.5 us
    psum x1, blocking collectives, per_device(): error_sum = lax.psum(local_error, 'space')  33.2 us
    all_gather x1, waiting for transfers between devices, per_device(): full_one = lax.all_gather(hidden_one, 'tensor', axis=1, tiled=True)  30.2 us
    all_gather x1, waiting for transfers between devices, per_device(): full_two = lax.all_gather(hidden_two, 'tensor', axis=1, tiled=True)  23.1 us
    all_to_all x1, blocking collectives, per_device(): lax.all_to_all(second_weight, 'tensor', split_axis=0, concat_axis=1, tile...  22.7 us
    all_to_all x1, waiting for transfers between devices, per_device(): lax.all_to_all(first_weight, 'tensor', split_axis=0, concat_axis=1, tiled...  22.4 us
  transfers between devices with their start and end apart: 9, of which 7 were waited for; matrix products, arithmetic and copies ran while one was open for 7% of the time, Pallas kernels for 0%

commit v1 on v0

--- a/solution.py
+++ b/solution.py
@@ -1,14 +1,18 @@
+import functools
 import math
 
 import jax
 import jax.numpy as jnp
 from jax import lax
+from jax.experimental import pallas as pl
+from jax.experimental.pallas import tpu as pltpu
 from jax.sharding import PartitionSpec as P
 
-V = 88
 PP = 4
 PROW_DEV = 4
 LONP = 224
+MESH = pl.DeviceIdType.MESH
+VMEM = pl.BlockSpec(memory_space=pltpu.VMEM)
 
 
 def slope(z):
@@ -16,6 +20,372 @@
     return cdf + z * jnp.exp(-0.5 * z * z) / math.sqrt(2.0 * math.pi)
 
 
+def flipped(s, bit):
+    step = 1 << bit
+    return s + step - 2 * step * ((s // step) % 2)
+
+
+def greet(partners):
+    barrier = pltpu.get_barrier_semaphore()
+    for partner in partners:
+        pl.semaphore_signal(barrier, inc=1, device_id=partner, device_id_type=MESH)
+    pl.semaphore_wait(barrier, len(partners))
+
+
+def params(number):
+    return pltpu.CompilerParams(
+        collective_id=number, has_side_effects=True, vmem_limit_bytes=60 * 2**20
+    )
+
+
+def gather_kernel(
+    tok, one, two, head, tar, o_tok, o_one, o_two, o_head, o_tar, send, recv, local
+):
+    s, x = lax.axis_index("space"), lax.axis_index("tensor")
+    other = 1 - x
+    across, core, along = (s, other), (flipped(s, 0), x), (flipped(s, 1), x)
+    quarter = s % 4
+    beyond = (quarter + 2) % 4
+    width = one.shape[1]
+    rows = one.shape[0] // 4
+    cols = head.shape[1] // 4
+    half = o_tok.shape[0]
+
+    def span(index, size):
+        return pl.ds(pl.multiple_of(index * size, size), size)
+
+    sources = [
+        one.at[span(quarter, rows), :],
+        two.at[span(quarter, rows), :],
+        head.at[:, span(quarter, cols)],
+    ]
+    places = [
+        lambda side, q: o_one.at[span(q, rows), span(side, width)],
+        lambda side, q: o_two.at[span(q, rows), span(side, width)],
+        lambda side, q: o_head.at[side, :, span(q, cols)],
+    ]
+
+    greet([across, core, along])
+
+    def remote(src, dst, slot, target):
+        copy = pltpu.make_async_remote_copy(
+            src_ref=src,
+            dst_ref=dst,
+            send_sem=send.at[slot],
+            recv_sem=recv.at[slot],
+            device_id=target,
+            device_id_type=MESH,
+        )
+        copy.start()
+        return copy
+
+    firsts = [remote(sources[k], places[k](x, quarter), k, across) for k in range(3)]
+    extra = [
+        remote(tok.at[span(other, half), :], o_tok.at[:, span(x, width)], 12, across),
+        remote(tar.at[other], o_tar.at[x], 13, across),
+    ]
+    own = [
+        pltpu.make_async_copy(one, o_one.at[:, span(x, width)], local.at[0]),
+        pltpu.make_async_copy(two, o_two.at[:, span(x, width)], local.at[1]),
+        pltpu.make_async_copy(head, o_head.at[x], local.at[2]),
+        pltpu.make_async_copy(tok.at[span(x, half), :], o_tok.at[:, span(x, width)], local.at[3]),
+        pltpu.make_async_copy(tar.at[x], o_tar.at[x], local.at[4]),
+    ]
+    for copy in own:
+        copy.start()
+    cores, alongs, lasts = [], [], []
+
+    def forward(k):
+        firsts[k].wait_recv()
+        piece = places[k](other, quarter)
+        alongs.append(remote(piece, piece, 3 + k, along))
+        cores.append(remote(piece, piece, 6 + k, core))
+
+    def finish(k):
+        alongs[k].wait_recv()
+        piece = places[k](other, beyond)
+        lasts.append(remote(piece, piece, 9 + k, core))
+
+    forward(0)
+    forward(1)
+    finish(0)
+    forward(2)
+    finish(1)
+    finish(2)
+    for copy in cores + lasts + extra:
+        copy.wait_recv()
+    for copy in firsts + alongs + cores + lasts + extra:
+        copy.wait_send()
+    for copy in own:
+        copy.wait()
+
+
+def gather(tokens, first, second, head, targets):
+    count, width = tokens.shape
+    half = count // 2
+    shape = jax.ShapeDtypeStruct
+    return pl.pallas_call(
+        gather_kernel,
+        out_shape=(
+            shape((half, 2 * width), tokens.dtype),
+            shape((first.shape[0], 2 * first.shape[1]), first.dtype),
+            shape((second.shape[0], 2 * second.shape[1]), second.dtype),
+            shape((2,) + head.shape, head.dtype),
+            shape(targets.shape, targets.dtype),
+        ),
+        in_specs=[VMEM] * 5,
+        out_specs=[VMEM] * 5,
+        scratch_shapes=[
+            pltpu.SemaphoreType.DMA((14,)),
+            pltpu.SemaphoreType.DMA((14,)),
+            pltpu.SemaphoreType.DMA((5,)),
+        ],
+        compiler_params=params(0),
+        name="gather",
+    )(tokens, first, second, head, targets)
+
+
+def total_kernel(groups, v_ref, o_ref, near, far, mid, send, recv):
+    s, x = lax.axis_index("space"), lax.axis_index("tensor")
+    low, high = s % 4, s // 4
+    mine = x * 4 + low
+
+    def near_peer(d):
+        j = (mine + d) % 8
+        return (high * 4 + j % 4, j // 4)
+
+    def far_peer(d):
+        return (((high + d) % groups) * 4 + low, x)
+
+    greet([near_peer(d) for d in range(1, 8)] + [far_peer(d) for d in range(1, groups)])
+
+    def share(src, slots, me, peers, base):
+        copies = []
+        for n, peer in enumerate(peers):
+            copy = pltpu.make_async_remote_copy(
+                src_ref=src,
+                dst_ref=slots.at[me],
+                send_sem=send.at[base + n],
+                recv_sem=recv.at[base + n],
+                device_id=peer,
+                device_id_type=MESH,
+            )
+            copy.start()
+            copies.append(copy)
+        slots[me] = src[...]
+        for copy in copies:
+            copy.wait()
+
+    share(v_ref, near, mine, [near_peer(d) for d in range(1, 8)], 0)
+    mid[...] = jnp.sum(near[...], axis=0)
+    share(mid, far, high, [far_peer(d) for d in range(1, groups)], 7)
+    o_ref[...] = jnp.sum(far[...], axis=0)
+
+
+def total(values):
+    groups = lax.axis_size("space") // 4
+    return pl.pallas_call(
+        functools.partial(total_kernel, groups),
+        out_shape=jax.ShapeDtypeStruct(values.shape, values.dtype),
+        in_specs=[VMEM],
+        out_specs=VMEM,
+        scratch_shapes=[
+            pltpu.VMEM((8,) + values.shape, values.dtype),
+            pltpu.VMEM((groups,) + values.shape, values.dtype),
+            pltpu.VMEM(values.shape, values.dtype),
+            pltpu.SemaphoreType.DMA((6 + groups,)),
+            pltpu.SemaphoreType.DMA((6 + groups,)),
+        ],
+        compiler_params=params(1),
+        name="total",
+    )(values)
+
+
+X = -1
+
+
+def orders(bits):
+    rest = list(range(3, bits))
+    return ([0, 1, 2, X] + rest, [0, 2, 1, X] + rest, [0, X, 1, 2] + rest)
+
+
+def pieces(bits, order, shape):
+    found = []
+    left = list(range(bits))[::-1]
+    rows, cols = shape
+    for bit in order:
+        if bit == X:
+            cols //= 2
+        else:
+            left.remove(bit)
+        found.append((2,) * len(left) + (rows, cols))
+    return found
+
+
+def scatter_kernel(bits, steps, *refs):
+    (g_one, g_two, g_head, tok), refs = refs[:4], refs[4:]
+    (outs, o_tok), refs = (refs[:3], refs[3]), refs[4:]
+    count = bits + 1
+    landing = [refs[count * k : count * (k + 1)] for k in range(3)]
+    refs = refs[3 * count :]
+    kept = [refs[bits * k : bits * (k + 1)] for k in range(3)]
+    send, recv = refs[3 * bits :]
+    s, x = lax.axis_index("space"), lax.axis_index("tensor")
+
+    def peer(bit):
+        return (s, 1 - x) if bit == X else (flipped(s, bit), x)
+
+    def part(ref, left, bit, near):
+        if bit == X:
+            width = ref.shape[-1] // 2
+            side = x if near else 1 - x
+            place = pl.ds(pl.multiple_of(side * width, width), width)
+            return (slice(None),) * (len(ref.shape) - 1) + (place,)
+        value = (s // (1 << bit)) % 2
+        value = value if near else 1 - value
+        return (slice(None),) * left.index(bit) + (value,)
+
+    greet([peer(b) for b in [X] + list(range(bits))])
+
+    def start(k, n, ref, left):
+        bit = steps[k][n]
+        copy = pltpu.make_async_remote_copy(
+            src_ref=ref.at[part(ref, left, bit, False)],
+            dst_ref=landing[k][n],
+            send_sem=send.at[k * count + n],
+            recv_sem=recv.at[k * count + n],
+            device_id=peer(bit),
+            device_id_type=MESH,
+        )
+        copy.start()
+        return copy
+
+    state = []
+    for k, ref in ((1, g_two), (0, g_one), (2, g_head)):
+        left = list(range(bits))[::-1]
+        state.append([k, ref, left, start(k, 0, ref, left)])
+    width = tok.shape[1] // 2
+    tail = pltpu.make_async_remote_copy(
+        src_ref=tok.at[:, pl.ds(pl.multiple_of((1 - x) * width, width), width)],
+        dst_ref=o_tok,
+        send_sem=send.at[3 * count],
+        recv_sem=recv.at[3 * count],
+        device_id=peer(X),
+        device_id_type=MESH,
+    )
+    tail.start()
+    copies = [tail]
+    for n in range(count):
+        for entry in state:
+            k, ref, left, copy = entry
+            bit = steps[k][n]
+            copies.append(copy)
+            copy.wait_recv()
+            mine = ref[part(ref, left, bit, True)].astype(jnp.float32)
+            both = mine + landing[k][n][...].astype(jnp.float32)
+            if n == count - 1:
+                outs[k][...] = both
+                continue
+            target = kept[k][n]
+            target[...] = both.astype(target.dtype)
+            left = [b for b in left if b != bit]
+            entry[1:] = [target, left, start(k, n + 1, target, left)]
+    tail.wait_recv()
+    for copy in copies:
+        copy.wait_send()
+
+
+def scatter(g_one, g_two, g_head, tok):
+    size = lax.axis_size("space")
+    bits = size.bit_length() - 1
+    steps = orders(bits)
+    inputs = [g.reshape((2,) * bits + (g.shape[0] // size, g.shape[1])) for g in (g_one, g_two, g_head)]
+    shapes = [pieces(bits, steps[k], inputs[k].shape[-2:]) for k in range(3)]
+    low = jnp.bfloat16
+    scratch = [pltpu.VMEM(shape, low) for k in range(3) for shape in shapes[k]]
+    scratch += [pltpu.VMEM(shape, low) for k in range(3) for shape in shapes[k][:-1]]
+    slots = 3 * (bits + 1) + 1
+    return pl.pallas_call(
+        functools.partial(scatter_kernel, bits, steps),
+        out_shape=tuple(jax.ShapeDtypeStruct(shapes[k][-1], jnp.float32) for k in range(3))
+        + (jax.ShapeDtypeStruct((tok.shape[0], tok.shape[1] // 2), tok.dtype),),
+        in_specs=[VMEM] * 4,
+        out_specs=[VMEM] * 4,
+        scratch_shapes=scratch
+        + [pltpu.SemaphoreType.DMA((slots,)), pltpu.SemaphoreType.DMA((slots,))],
+        compiler_params=params(2),
+        name="scatter",
+    )(*inputs, tok)
+
+
+def mix(a, b, dims):
+    return lax.dot_general(a, b, ((dims[:1], dims[1:]), ((), ())), preferred_element_type=jnp.float32)
+
+
+def per_device(
+    tokens, first_weight, second_weight, head_weight, targets, land_mask, variable_kind, loss_scale
+):
+    low = jnp.bfloat16
+    count, width = tokens.shape
+    half = count // 2
+    rows = head_weight.shape[0]
+    kinds = 2 * rows // PP
+    s, x = lax.axis_index("space"), lax.axis_index("tensor")
+    lanes = -(-(half + 1) // 128) * 128
+    sent = jnp.stack([targets[:, :half], targets[:, half:]]).astype(low)
+    label = jnp.repeat(variable_kind, PP).astype(low)[None, :, None]
+    label = jnp.broadcast_to(label, (2, rows, lanes - half))
+    sent = jnp.concatenate([sent, label], axis=2)
+    toks, w_one, w_two, w_head, seen = gather(
+        tokens, first_weight, second_weight, head_weight, sent
+    )
+    w_head = w_head.reshape(2 * rows, -1)
+    goal = seen[:, :, :half].reshape(kinds, PP, half)
+    kind = seen[:, :, half].reshape(kinds, PP)[:, :, None]
+
+    position = s * count + x * half + jnp.arange(half, dtype=jnp.int32)
+    cell = jnp.arange(PP, dtype=jnp.int32)
+    lat_row = 2 * (position // LONP)[None, :] + (cell // 2)[:, None]
+    nlat = 2 * PROW_DEV * lax.axis_size("space")
+    cell_weight = jnp.cos(math.pi / 2.0 * (lat_row.astype(jnp.float32) + 0.5) / nlat)
+    land = lax.dynamic_slice_in_dim(land_mask, x * half, half, 1).astype(jnp.float32)
+    valid = jnp.where(kind == 0, 1.0, jnp.where(kind == 1, land[None], 1.0 - land[None]))
+    masked = cell_weight[None] * valid
+
+    pre_one = mix(toks, w_one, (1, 0))
+    hidden_one = jax.nn.gelu(pre_one, approximate=False).astype(low)
+    pre_two = mix(hidden_one, w_two, (1, 0))
+    hidden_two = jax.nn.gelu(pre_two, approximate=False).astype(low)
+    predicted = mix(w_head, hidden_two, (1, 1))
+    error = predicted.reshape(kinds, PP, half) - goal.astype(jnp.float32)
+    scored = masked * error
+    sums = jnp.stack([jnp.sum(scored * error, axis=(1, 2)), jnp.sum(masked, axis=(1, 2))])
+    wide = -(-kinds // 128) * 128
+    sums = total(jnp.pad(sums, ((0, 6), (0, wide - kinds))))
+    weight_sum = sums[1, :kinds]
+    root = jnp.sqrt(sums[0, :kinds] / weight_sum + 1e-06)
+    loss = jnp.sum(root) / kinds
+    coef = loss_scale / (kinds * root * weight_sum)
+    grad_pred = (coef[:, None, None] * scored).reshape(kinds * PP, half).astype(low)
+
+    head_term = mix(hidden_two, grad_pred, (0, 1)).astype(low)
+    pad = jnp.zeros((head_term.shape[0], -rows % 128), low)
+    head_term = jnp.concatenate([head_term[:, :rows], pad, head_term[:, rows:], pad], axis=1)
+    grad_two = (mix(grad_pred, w_head, (0, 0)) * slope(pre_two)).astype(low)
+    second_term = mix(hidden_one, grad_two, (0, 0)).astype(low)
+    grad_one = (mix(grad_two, w_two, (1, 1)) * slope(pre_one)).astype(low)
+    first_term = mix(toks, grad_one, (0, 0)).astype(low)
+    token_term = mix(grad_one, w_one, (1, 1)).astype(low)
+    first_grad, second_grad, head_grad, arrived = scatter(
+        first_term, second_term, head_term, token_term
+    )
+    kept = lax.dynamic_slice_in_dim(token_term, x * width, width, 1)
+    upper = jnp.where(x == 0, kept, arrived)
+    lower = jnp.where(x == 0, arrived, kept)
+    token_grad = jnp.concatenate([upper, lower], axis=0).astype(jnp.float32)
+    return (loss, token_grad, first_grad, second_grad, head_grad[:, :rows].T)
+
+
 def column_folder(weights, piece):
     return lax.dot_general(
         piece, weights, (((1,), (1,)), ((), ())), preferred_element_type=jnp.float32
@@ -28,7 +398,7 @@
     )
 
 
-def per_device(
+def per_device_wide(
     tokens, first_weight, second_weight, head_weight, targets, land_mask, variable_kind, loss_scale
 ):
     count = tokens.shape[0]
@@ -64,8 +434,8 @@
     local_error = jnp.sum(masked * error * error, axis=(1, 2))
     error_sum = lax.psum(local_error, "space")
     root = jnp.sqrt(error_sum / weight_sum + 1e-06)
-    loss = lax.psum(jnp.sum(root), "tensor") / V
-    coef = loss_scale / (V * root * weight_sum)
+    loss = lax.psum(jnp.sum(root), "tensor") / (kinds * lax.axis_size("tensor"))
+    coef = loss_scale / (kinds * lax.axis_size("tensor") * root * weight_sum)
     grad_pred = (
         (coef[:, None, None] * masked * error).reshape(kinds * PP, count).astype(jnp.bfloat16)
     )
@@ -98,8 +468,10 @@
 
 
 def solution(mesh):
+    size = mesh.shape["space"]
+    paired = mesh.shape["tensor"] == 2 and size >= 8 and size & (size - 1) == 0
     return jax.shard_map(
-        per_device,
+        per_device if paired else per_device_wide,
         mesh=mesh,
         in_specs=(
             P("space", "tensor"),

time: 391 us -> 138 us (0.35)
  waiting for transfers between devices: 245 us -> 0 us
  Pallas kernels: 0 us -> 90.7 us
  blocking collectives: 69.1 us -> 0 us
  between operations: 16.8 us -> 3.38 us
  starting transfers between devices: 8.16 us -> 0 us
  matrix products: 36.5 us -> 28.4 us
  other arithmetic: 4.37 us -> 8.88 us
  local copies, waits for them, and re-layouts: 10.7 us -> 6.19 us
    all_gather x5 -> x0, waiting for transfers between devices: 96.4 us -> none  [the longest x1 34.5 us: per_device(): full_in = lax.all_gather(tokens, 'tensor', axis=1, tiled=True)]
    pallas_call x0 -> x3, Pallas kernels: none -> 90.7 us  [the longest x1 42.8 us: scatter(): pl.pallas_call(functools.partial(scatter_kernel, bits, steps), out_shape=...]
    unnamed x8 -> x0, waiting for transfers between devices: 66.7 us -> none
    reduce_scatter x1 -> x0, waiting for transfers between devices: 59.2 us -> none  [per_device(): lax.psum_scatter(head_term, 'space', scatter_dimension=1, tiled=True)]
    psum x2 -> x0, blocking collectives: 38.8 us -> none  [the longest x1 33.2 us: per_device(): error_sum = lax.psum(local_error, 'space')]
    all_to_all x1 -> x0, blocking collectives: 22.7 us -> none  [per_device(): lax.all_to_all(second_weight, 'tensor', split_axis=0, concat_axis=1, tile...]
    all_to_all x2 -> x0, waiting for transfers between devices: 22.4 us -> none  [the longest x1 22.4 us: per_device(): lax.all_to_all(first_weight, 'tensor', split_axis=0, concat_axis=1, tiled...]
    dot_general x9, matrix products: 36.5 us -> 28.4 us  [mix(): lax.dot_general(a, b, ((dims[:1], dims[1:]), ((), ())), preferred_element...]
  transfers between devices with their start and end apart: 9 -> 0, of which waited for: 7 -> 0; matrix products, arithmetic and copies ran while one was open for 7% -> 0% of each run, Pallas kernels for 0% -> 0%
where the time goes in v1:
time: 138 us
  Pallas kernels  90.7 us (66%)
  matrix products  28.4 us (21%)
  other arithmetic  8.88 us (6%)
  local copies, waits for them, and re-layouts  6.19 us (4%)
  between operations  3.38 us (2%)
    pallas_call x1, Pallas kernels, scatter(): pl.pallas_call(functools.partial(scatter_kernel, bits, steps), out_shape=...  42.8 us
    pallas_call x1, Pallas kernels, gather(): pl.pallas_call(gather_kernel, out_shape=(shape((half, 2 * width), tokens....  36.7 us
    dot_general x9, matrix products, mix(): lax.dot_general(a, b, ((dims[:1], dims[1:]), ((), ())), preferred_element...  28.4 us
    pallas_call x1, Pallas kernels, total(): pl.pallas_call(functools.partial(total_kernel, groups), out_shape=jax.Sha...  11.2 us

profile of v1, /device:TPU:0, one launch (start us, length us, event | category | flops | bytes accessed | tf_op | source)
XLA Modules:
  0.0 137.5 jit_solution(10653881932956416661)
XLA Ops:
  0.7 0.9 broadcast_subtract_fusion
  1.5 1.1 convert.9
  2.8 0.7 convert_element_type.65
  3.7 0.8 pad_maximum_fusion.1.tar
  4.6 36.7 %gather.1 = (bf16[448,1024]{1,0:T(8,128)(2,1)}, bf16[1024,1024]{1,0:T(8,128)(2,1)}, bf16[1024,1024]{1,0:T(8,128)(2,1)}, bf16[2,176,1024]{2,1,0:T(8,128)(2,1)}, bf16[2,176,512]{2,1,0:T(8,128)(2,1)}) custom-call(bf16[896,512]{1,0:T(8,128)(2,1)} %tok.1, bf16[1024,512]{1,0:T(8,128)(2,1)} %one.1, bf16[1024,512]{1,0:T(8,128)(2,1)} %two.1, bf16[176,1024]{1,0:T(8,128)(2,1)} %head.1, ...), custom_call_target="tpu_custom_call" | custom-call | tf_op jit(solution)/shard_map/gather/pallas_call | solution.py:127
  41.3 7.9 %fusion.2 = (bf16[448,1024]{1,0:T(8,128)(2,1)S(1)}, f32[448,1024]{1,0:T(8,128)}) fusion(bf16[448,1024]{1,0:T(8,128)(2,1)} %get-tuple-element.16, bf16[1024,1024]{1,0:T(8,128)(2,1)} %get-tuple-element.17), kind=kOutput, calls=%fused_computation.8 | convolution fusion | flops 969342976 | bytes 5767168 | tf_op jit(solution)/shard_map/dot_general | solution.py:322
  49.2 6.1 %fusion.5 = (bf16[448,1024]{1,0:T(8,128)(2,1)}, f32[448,1024]{1,0:T(8,128)}) fusion(bf16[448,1024]{1,0:T(8,128)(2,1)S(1)} %get-tuple-element.37, bf16[1024,1024]{1,0:T(8,128)(2,1)S(1)} %copy-done.7), kind=kOutput, calls=%fused_computation.11 | convolution fusion | flops 969342976 | bytes 5767168 | tf_op jit(solution)/shard_map/dot_general | solution.py:322
  56.7 2.2 %multiply_reduce_fusion = (f32[88]{0:T(128)S(1)}, f32[88]{0:T(128)S(1)}, f32[88,4,448]{2,0,1:T(8,128)S(1)}) fusion(f32[4,448]{1,0:T(4,128)S(1)} %get-tuple-element.29, f32[4,448]{1,0:T(4,128)S(1)} %get-tuple-element.30, f32[4,448]{1,0:T(4,128)S(1)} %get-tuple-element.42, pred[88,4]{0,1:T(4,128)(4,1)S(1)} %copy.19, pred[88,4]{0,1:T(4,128)(4,1)S(1)} %copy.18, ...), kind=kOutput, calls=%fused_computation.62 | convolution fusion | flops 324222784 | bytes 2922880 | tf_op jit(solution)/shard_map/dot_general | solution.py:322
  58.9 0.6 select_maximum_fusion.v_ref
  59.5 11.2 %total.1 = f32[8,128]{1,0:T(8,128)} custom-call(f32[8,128]{1,0:T(8,128)} %select_maximum_fusion.v_ref), custom_call_target="tpu_custom_call" | custom-call | tf_op jit(solution)/shard_map/total/pallas_call | solution.py:187
  71.3 0.8 fusion.38
  72.7 1.1 fusion.11
  74.3 0.6 copy-done.14
  74.9 1.9 %fusion.17 = bf16[448,1024]{1,0:T(8,128)(2,1)S(1)} fusion(f32[448,1024]{1,0:T(8,128)S(1)} %copy-done.14, bf16[448,1024]{1,0:T(8,128)(2,1)S(1)} %fusion.11, bf16[1024,1024]{1,0:T(8,128)(2,1)S(1)} %copy-done.8), kind=kOutput, calls=%fused_computation.23 | convolution fusion | flops 944111616 | bytes 5767168 | tf_op jit(solution)/shard_map/dot_general | solution.py:322
  76.9 2.1 %convolution_convert_fusion.2.refs_3_ = bf16[448,1024]{1,0:T(8,128)(2,1)} fusion(bf16[448,1024]{1,0:T(8,128)(2,1)S(1)} %fusion.17, bf16[1024,1024]{1,0:T(8,128)(2,1)S(1)} %copy-done.6), kind=kOutput, calls=%fused_computation.54 | convolution fusion | flops 939982848 | bytes 3932160 | tf_op jit(solution)/shard_map/dot_general | solution.py:322
  79.8 1.3 copy.23
  81.1 3.9 %convolution_convert_fusion = bf16[1024,1024]{1,0:T(8,128)(2,1)} fusion(bf16[448,1024]{1,0:T(8,128)(2,1)} %copy-done.15, bf16[448,1024]{1,0:T(8,128)(2,1)S(1)} %copy-done.13), kind=kOutput, calls=%fused_computation.4 | convolution fusion | flops 940572672 | bytes 3932160 | tf_op jit(solution)/shard_map/dot_general | solution.py:322
  85.0 2.6 %convolution_convert_fusion.1 = bf16[1024,1024]{1,0:T(8,128)(2,1)} fusion(bf16[448,1024]{1,0:T(8,128)(2,1)S(1)} %copy-done.9, bf16[448,1024]{1,0:T(8,128)(2,1)S(1)} %fusion.17), kind=kOutput, calls=%fused_computation.5 | convolution fusion | flops 940572672 | bytes 3932160 | tf_op jit(solution)/shard_map/dot_general | solution.py:322
  87.6 42.8 %scatter.1 = (f32[64,512]{1,0:T(8,128)}, f32[64,512]{1,0:T(8,128)}, f32[64,256]{1,0:T(8,128)}, bf16[448,512]{1,0:T(8,128)(2,1)}) custom-call(bf16[2,2,2,2,64,1024]{5,4,3,2,1,0:T(8,128)(2,1)} %bitcast.48, bf16[2,2,2,2,64,1024]{5,4,3,2,1,0:T(8,128)(2,1)} %bitcast.47, bf16[2,2,2,2,64,512]{5,4,3,2,1,0:T(8,128)(2,1)} %bitcast.46, ...), custom_call_target="tpu_custom_call" | custom-call | tf_op jit(solution)/shard_map/scatter/pallas_call | solution.py:308
  130.5 1.2 broadcast_select_fusion.1
  131.7 1.5 %maximum_convert_fusion = f32[896,512]{1,0:T(8,128)} fusion(bf16[448,512]{1,0:T(8,128)(2,1)S(1)} %get-tuple-element.32, bf16[448,512]{1,0:T(8,128)(2,1)S(1)} %get-tuple-element.31), kind=kLoop, calls=%fused_computation.58 | loop fusion | flops 1835008 | bytes 2752512 | tf_op jit(solution)/shard_map/convert_element_type | solution.py:385
  133.2 0.6 slice_bitcast_fusion.2
  135.1 0.7 copy.32
  135.7 0.7 copy.33
  (53 shorter events, 4.2 us)
Async XLA Ops:
  41.3 7.9 %copy-start.7 = (bf16[1024,1024]{1,0:T(8,128)(2,1)S(1)}, bf16[1024,1024]{1,0:T(8,128)(2,1)}, u32[]{:S(2)}) copy-start(bf16[1024,1024]{1,0:T(8,128)(2,1)} %get-tuple-element.18) | copy-start | bytes 6291460
  49.2 6.1 %copy-start.15 = (bf16[448,1024]{1,0:T(8,128)(2,1)}, bf16[448,1024]{1,0:T(8,128)(2,1)S(1)}, u32[]{:S(2)}) copy-start(bf16[448,1024]{1,0:T(8,128)(2,1)S(1)} %get-tuple-element.37) | copy-start | bytes 2752516
  49.2 6.1 %copy-start.2 = (bf16[2,176,512]{2,1,0:T(8,128)(2,1)S(1)}, bf16[2,176,512]{2,1,0:T(8,128)(2,1)}, u32[]{:S(2)}) copy-start(bf16[2,176,512]{2,1,0:T(8,128)(2,1)} %get-tuple-element.14) | copy-start | bytes 1081348
  55.3 1.1 copy-start.1
  58.8 13.8 %copy-start.11 = (f32[448,1024]{1,0:T(8,128)S(1)}, f32[448,1024]{1,0:T(8,128)}, u32[]{:S(2)}) copy-start(f32[448,1024]{1,0:T(8,128)} %get-tuple-element.40) | copy-start | bytes 5505028
  72.7 1.6 %copy-start.8 = (bf16[1024,1024]{1,0:T(8,128)(2,1)S(1)}, bf16[1024,1024]{1,0:T(8,128)(2,1)}, u32[]{:S(2)}) copy-start(bf16[1024,1024]{1,0:T(8,128)(2,1)} %get-tuple-element.18) | copy-start | bytes 6291460
  72.7 2.2 %copy-start.14 = (f32[448,1024]{1,0:T(8,128)S(1)}, f32[448,1024]{1,0:T(8,128)}, u32[]{:S(2)}) copy-start(f32[448,1024]{1,0:T(8,128)} %get-tuple-element.38) | copy-start | bytes 5505028
  73.8 3.0 %copy-start.12 = (bf16[448,1024]{1,0:T(8,128)(2,1)}, bf16[448,1024]{1,0:T(8,128)(2,1)S(1)}, u32[]{:S(2)}) copy-start(bf16[448,1024]{1,0:T(8,128)(2,1)S(1)} %fusion.11) | copy-start | bytes 2752516
  74.9 1.9 %copy-start.6 = (bf16[1024,1024]{1,0:T(8,128)(2,1)S(1)}, bf16[1024,1024]{1,0:T(8,128)(2,1)}, u32[]{:S(2)}) copy-start(bf16[1024,1024]{1,0:T(8,128)(2,1)} %get-tuple-element.17) | copy-start | bytes 6291460
  76.9 2.1 %copy-start.10 = (bf16[448,1024]{1,0:T(8,128)(2,1)S(1)}, bf16[448,1024]{1,0:T(8,128)(2,1)}, u32[]{:S(2)}) copy-start(bf16[448,1024]{1,0:T(8,128)(2,1)} %get-tuple-element.39) | copy-start | bytes 2752516
  79.6 1.4 %copy-start.13 = (bf16[448,1024]{1,0:T(8,128)(2,1)S(1)}, bf16[448,1024]{1,0:T(8,128)(2,1)}, u32[]{:S(2)}) copy-start(bf16[448,1024]{1,0:T(8,128)(2,1)} %copy-done.12) | copy-start | bytes 2752516
  81.1 3.9 %copy-start.9 = (bf16[448,1024]{1,0:T(8,128)(2,1)S(1)}, bf16[448,1024]{1,0:T(8,128)(2,1)}, u32[]{:S(2)}) copy-start(bf16[448,1024]{1,0:T(8,128)(2,1)} %get-tuple-element.16) | copy-start | bytes 2752516
  87.6 42.8 %copy-start = (bf16[448,1024]{1,0:T(8,128)(2,1)S(1)}, bf16[448,1024]{1,0:T(8,128)(2,1)}, u32[]{:S(2)}) copy-start(bf16[448,1024]{1,0:T(8,128)(2,1)} %convolution_convert_fusion.2.refs_3_) | copy-start | bytes 2752516
  131.7 1.5 %copy-start.5 = (f32[64,256]{1,0:T(8,128)S(1)}, f32[64,256]{1,0:T(8,128)}, u32[]{:S(2)}) copy-start(f32[64,256]{1,0:T(8,128)} %get-tuple-element.22) | copy-start | bytes 196612
  131.7 3.4 %copy-start.4 = (f32[64,512]{1,0:T(8,128)S(1)}, f32[64,512]{1,0:T(8,128)}, u32[]{:S(2)}) copy-start(f32[64,512]{1,0:T(8,128)} %get-tuple-element.50) | copy-start | bytes 393220
  131.7 4.0 %copy-start.3 = (f32[64,512]{1,0:T(8,128)S(1)}, f32[64,512]{1,0:T(8,128)}, u32[]{:S(2)}) copy-start(f32[64,512]{1,0:T(8,128)} %get-tuple-element.51) | copy-start | bytes 393220

commit v2 on v1

--- a/solution.py
+++ b/solution.py
@@ -15,6 +15,10 @@
 VMEM = pl.BlockSpec(memory_space=pltpu.VMEM)
 
 
+def bent(z):
+    return (0.5 * z * (1.0 + lax.erf(z / math.sqrt(2.0)))).astype(jnp.bfloat16)
+
+
 def slope(z):
     cdf = 0.5 * (1.0 + lax.erf(z / math.sqrt(2.0)))
     return cdf + z * jnp.exp(-0.5 * z * z) / math.sqrt(2.0 * math.pi)
@@ -43,21 +47,20 @@
 ):
     s, x = lax.axis_index("space"), lax.axis_index("tensor")
     other = 1 - x
-    across, core, along = (s, other), (flipped(s, 0), x), (flipped(s, 1), x)
-    quarter = s % 4
-    beyond = (quarter + 2) % 4
+    across, core, along, up = (s, other), (flipped(s, 0), x), (flipped(s, 1), x), (flipped(s, 2), x)
+    mine = s % 8
     width = one.shape[1]
-    rows = one.shape[0] // 4
-    cols = head.shape[1] // 4
+    rows = one.shape[0] // 8
+    cols = head.shape[1] // 8
     half = o_tok.shape[0]
 
     def span(index, size):
         return pl.ds(pl.multiple_of(index * size, size), size)
 
     sources = [
-        one.at[span(quarter, rows), :],
-        two.at[span(quarter, rows), :],
-        head.at[:, span(quarter, cols)],
+        one.at[span(mine, rows), :],
+        two.at[span(mine, rows), :],
+        head.at[:, span(mine, cols)],
     ]
     places = [
         lambda side, q: o_one.at[span(q, rows), span(side, width)],
@@ -65,7 +68,8 @@
         lambda side, q: o_head.at[side, :, span(q, cols)],
     ]
 
-    greet([across, core, along])
+    greet([across, core, along, up])
+    started = []
 
     def remote(src, dst, slot, target):
         copy = pltpu.make_async_remote_copy(
@@ -77,12 +81,13 @@
             device_id_type=MESH,
         )
         copy.start()
+        started.append(copy)
         return copy
 
-    firsts = [remote(sources[k], places[k](x, quarter), k, across) for k in range(3)]
+    firsts = [remote(sources[k], places[k](x, mine), 8 * k, across) for k in range(3)]
     extra = [
-        remote(tok.at[span(other, half), :], o_tok.at[:, span(x, width)], 12, across),
-        remote(tar.at[other], o_tar.at[x], 13, across),
+        remote(tok.at[span(other, half), :], o_tok.at[:, span(x, width)], 24, across),
+        remote(tar.at[other], o_tar.at[x], 25, across),
     ]
     own = [
         pltpu.make_async_copy(one, o_one.at[:, span(x, width)], local.at[0]),
@@ -93,28 +98,41 @@
     ]
     for copy in own:
         copy.start()
-    cores, alongs, lasts = [], [], []
-
-    def forward(k):
+
+    def pass_on(k, q, slot, target):
+        piece = places[k](other, q)
+        return remote(piece, piece, 8 * k + slot, target)
+
+    ups, alongs, beyonds, ends = {}, {}, {}, []
+
+    def stage_one(k):
         firsts[k].wait_recv()
-        piece = places[k](other, quarter)
-        alongs.append(remote(piece, piece, 3 + k, along))
-        cores.append(remote(piece, piece, 6 + k, core))
-
-    def finish(k):
+        ups[k] = pass_on(k, mine, 1, up)
+        alongs[k] = pass_on(k, mine, 2, along)
+        ends.append(pass_on(k, mine, 4, core))
+
+    def stage_two(k):
+        ups[k].wait_recv()
+        beyonds[k] = pass_on(k, flipped(mine, 2), 3, along)
+        ends.append(pass_on(k, flipped(mine, 2), 5, core))
+
+    def stage_three(k):
         alongs[k].wait_recv()
-        piece = places[k](other, beyond)
-        lasts.append(remote(piece, piece, 9 + k, core))
-
-    forward(0)
-    forward(1)
-    finish(0)
-    forward(2)
-    finish(1)
-    finish(2)
-    for copy in cores + lasts + extra:
+        ends.append(pass_on(k, flipped(mine, 1), 6, core))
+        beyonds[k].wait_recv()
+        ends.append(pass_on(k, flipped(flipped(mine, 1), 2), 7, core))
+
+    stage_one(0)
+    stage_one(1)
+    stage_two(0)
+    stage_one(2)
+    stage_two(1)
+    stage_two(2)
+    for k in range(3):
+        stage_three(k)
+    for copy in ends + extra:
         copy.wait_recv()
-    for copy in firsts + alongs + cores + lasts + extra:
+    for copy in started:
         copy.wait_send()
     for copy in own:
         copy.wait()
@@ -136,8 +154,8 @@
         in_specs=[VMEM] * 5,
         out_specs=[VMEM] * 5,
         scratch_shapes=[
-            pltpu.SemaphoreType.DMA((14,)),
-            pltpu.SemaphoreType.DMA((14,)),
+            pltpu.SemaphoreType.DMA((26,)),
+            pltpu.SemaphoreType.DMA((26,)),
             pltpu.SemaphoreType.DMA((5,)),
         ],
         compiler_params=params(0),
@@ -222,14 +240,17 @@
     return found
 
 
-def scatter_kernel(bits, steps, *refs):
-    (g_one, g_two, g_head, tok), refs = refs[:4], refs[4:]
-    (outs, o_tok), refs = (refs[:3], refs[3]), refs[4:]
+def scatter_kernel(bits, plan, *refs):
+    grads, tok, refs = refs[:3], refs[3], refs[4:]
+    outs, o_tok, refs = refs[:3], refs[3], refs[4:]
     count = bits + 1
-    landing = [refs[count * k : count * (k + 1)] for k in range(3)]
-    refs = refs[3 * count :]
-    kept = [refs[bits * k : bits * (k + 1)] for k in range(3)]
-    send, recv = refs[3 * bits :]
+    parts = len(plan)
+    landing = [refs[count * k : count * (k + 1)] for k in range(parts)]
+    refs = refs[parts * count :]
+    away = [refs[bits * k : bits * (k + 1)] for k in range(parts)]
+    refs = refs[parts * bits :]
+    kept = [refs[bits * k : bits * (k + 1)] for k in range(parts)]
+    send, recv = refs[parts * bits :]
     s, x = lax.axis_index("space"), lax.axis_index("tensor")
 
     def peer(bit):
@@ -246,50 +267,58 @@
         return (slice(None),) * left.index(bit) + (value,)
 
     greet([peer(b) for b in [X] + list(range(bits))])
-
-    def start(k, n, ref, left):
-        bit = steps[k][n]
+    copies = []
+
+    def start(k, n, src):
         copy = pltpu.make_async_remote_copy(
-            src_ref=ref.at[part(ref, left, bit, False)],
+            src_ref=src,
             dst_ref=landing[k][n],
             send_sem=send.at[k * count + n],
             recv_sem=recv.at[k * count + n],
-            device_id=peer(bit),
+            device_id=peer(plan[k][3][n]),
             device_id_type=MESH,
         )
         copy.start()
+        copies.append(copy)
         return copy
 
     state = []
-    for k, ref in ((1, g_two), (0, g_one), (2, g_head)):
+    for k, (which, first, rows, order) in enumerate(plan):
         left = list(range(bits))[::-1]
-        state.append([k, ref, left, start(k, 0, ref, left)])
+        ref = grads[which].at[(slice(None),) * bits + (pl.ds(first, rows),)]
+        copy = start(k, 0, ref.at[part(ref, left, order[0], False)])
+        left_now = [b for b in left if b != order[0]]
+        state.append((ref.at[part(ref, left, order[0], True)], left_now, copy))
     width = tok.shape[1] // 2
     tail = pltpu.make_async_remote_copy(
         src_ref=tok.at[:, pl.ds(pl.multiple_of((1 - x) * width, width), width)],
         dst_ref=o_tok,
-        send_sem=send.at[3 * count],
-        recv_sem=recv.at[3 * count],
+        send_sem=send.at[parts * count],
+        recv_sem=recv.at[parts * count],
         device_id=peer(X),
         device_id_type=MESH,
     )
     tail.start()
-    copies = [tail]
+    copies.append(tail)
+
+    def added(ref, arrived, index):
+        return ref[index].astype(jnp.float32) + arrived[index].astype(jnp.float32)
+
     for n in range(count):
-        for entry in state:
-            k, ref, left, copy = entry
-            bit = steps[k][n]
-            copies.append(copy)
+        for k, (which, first, rows, order) in enumerate(plan):
+            ref, left, copy = state[k]
+            arrived = landing[k][n]
             copy.wait_recv()
-            mine = ref[part(ref, left, bit, True)].astype(jnp.float32)
-            both = mine + landing[k][n][...].astype(jnp.float32)
             if n == count - 1:
-                outs[k][...] = both
+                outs[which][pl.ds(first, rows), :] = added(ref, arrived, ...)
                 continue
-            target = kept[k][n]
-            target[...] = both.astype(target.dtype)
-            left = [b for b in left if b != bit]
-            entry[1:] = [target, left, start(k, n + 1, target, left)]
+            bit = order[n + 1]
+            far = away[k][n]
+            far[...] = added(ref, arrived, part(arrived, left, bit, False)).astype(far.dtype)
+            copy = start(k, n + 1, far)
+            near = kept[k][n]
+            near[...] = added(ref, arrived, part(arrived, left, bit, True))
+            state[k] = (near, [b for b in left if b != bit], copy)
     tail.wait_recv()
     for copy in copies:
         copy.wait_send()
@@ -299,15 +328,25 @@
     size = lax.axis_size("space")
     bits = size.bit_length() - 1
     steps = orders(bits)
-    inputs = [g.reshape((2,) * bits + (g.shape[0] // size, g.shape[1])) for g in (g_one, g_two, g_head)]
-    shapes = [pieces(bits, steps[k], inputs[k].shape[-2:]) for k in range(3)]
-    low = jnp.bfloat16
-    scratch = [pltpu.VMEM(shape, low) for k in range(3) for shape in shapes[k]]
-    scratch += [pltpu.VMEM(shape, low) for k in range(3) for shape in shapes[k][:-1]]
-    slots = 3 * (bits + 1) + 1
+    grads = [g.reshape((2,) * bits + (g.shape[0] // size, g.shape[1])) for g in (g_one, g_two, g_head)]
+    rows = grads[0].shape[-2]
+    half = rows // 2
+    plan = [
+        (0, 0, half, steps[0]),
+        (1, 0, half, steps[1]),
+        (2, 0, rows, steps[2]),
+        (0, half, half, steps[0]),
+        (1, half, half, steps[1]),
+    ]
+    shapes = [pieces(bits, order, (n, grads[which].shape[-1])) for which, _, n, order in plan]
+    scratch = [pltpu.VMEM(shape, jnp.bfloat16) for found in shapes for shape in found]
+    scratch += [pltpu.VMEM(shape, jnp.bfloat16) for found in shapes for shape in found[1:]]
+    scratch += [pltpu.VMEM(shape, jnp.float32) for found in shapes for shape in found[1:]]
+    slots = len(plan) * (bits + 1) + 1
+    outs = [shapes[which][-1][-1] for which in range(3)]
     return pl.pallas_call(
-        functools.partial(scatter_kernel, bits, steps),
-        out_shape=tuple(jax.ShapeDtypeStruct(shapes[k][-1], jnp.float32) for k in range(3))
+        functools.partial(scatter_kernel, bits, plan),
+        out_shape=tuple(jax.ShapeDtypeStruct((rows, width), jnp.float32) for width in outs)
         + (jax.ShapeDtypeStruct((tok.shape[0], tok.shape[1] // 2), tok.dtype),),
         in_specs=[VMEM] * 4,
         out_specs=[VMEM] * 4,
@@ -315,7 +354,7 @@
         + [pltpu.SemaphoreType.DMA((slots,)), pltpu.SemaphoreType.DMA((slots,))],
         compiler_params=params(2),
         name="scatter",
-    )(*inputs, tok)
+    )(*grads, tok)
 
 
 def mix(a, b, dims):
@@ -353,9 +392,9 @@
     masked = cell_weight[None] * valid
 
     pre_one = mix(toks, w_one, (1, 0))
-    hidden_one = jax.nn.gelu(pre_one, approximate=False).astype(low)
+    hidden_one = bent(pre_one)
     pre_two = mix(hidden_one, w_two, (1, 0))
-    hidden_two = jax.nn.gelu(pre_two, approximate=False).astype(low)
+    hidden_two = bent(pre_two)
     predicted = mix(w_head, hidden_two, (1, 1))
     error = predicted.reshape(kinds, PP, half) - goal.astype(jnp.float32)
     scored = masked * error
@@ -380,9 +419,9 @@
         first_term, second_term, head_term, token_term
     )
     kept = lax.dynamic_slice_in_dim(token_term, x * width, width, 1)
-    upper = jnp.where(x == 0, kept, arrived)
-    lower = jnp.where(x == 0, arrived, kept)
-    token_grad = jnp.concatenate([upper, lower], axis=0).astype(jnp.float32)
+    side = lax.broadcasted_iota(jnp.int32, (2, half, width), 0)
+    token_grad = jnp.where(side == x, kept[None], arrived[None]).astype(jnp.float32)
+    token_grad = token_grad.reshape(count, width)
     return (loss, token_grad, first_grad, second_grad, head_grad[:, :rows].T)
 
 

time: 138 us -> 118 us (0.86)
  Pallas kernels: 90.7 us -> 78.7 us
  matrix products: 28.4 us -> 20.2 us
    dot_general x9, matrix products: 28.4 us -> 20.2 us  [mix(): lax.dot_general(a, b, ((dims[:1], dims[1:]), ((), ())), preferred_element...]
    pallas_call x1, Pallas kernels: 36.7 us -> 30.4 us  [gather(): pl.pallas_call(gather_kernel, out_shape=(shape((half, 2 * width), tokens....]
    pallas_call x1, Pallas kernels: 42.8 us -> 37.2 us  [scatter(): pl.pallas_call(functools.partial(scatter_kernel, bits, plan), out_shape=t...]
where the time goes in v2:
time: 118 us
  Pallas kernels  78.7 us (67%)
  matrix products  20.2 us (17%)
  other arithmetic  8.7 us (7%)
  local copies, waits for them, and re-layouts  6.67 us (6%)
  between operations  3.4 us (3%)
    pallas_call x1, Pallas kernels, scatter(): pl.pallas_call(functools.partial(scatter_kernel, bits, plan), out_shape=t...  37.2 us
    pallas_call x1, Pallas kernels, gather(): pl.pallas_call(gather_kernel, out_shape=(shape((half, 2 * width), tokens....  30.4 us
    dot_general x9, matrix products, mix(): lax.dot_general(a, b, ((dims[:1], dims[1:]), ((), ())), preferred_element...  20.2 us
    pallas_call x1, Pallas kernels, total(): pl.pallas_call(functools.partial(total_kernel, groups), out_shape=jax.Sha...  11.1 us
    unnamed x40, local copies, waits for them, and re-layouts  2.76 us
    convert_element_type x1, other arithmetic, per_device(): jnp.where(side == x, kept[None], arrived[None]).astype(jnp.float32)  2.48 us

profile of v2, /device:TPU:0, one launch (start us, length us, event | category | flops | bytes accessed | tf_op | source)
XLA Modules:
  0.0 117.7 jit_solution(12127426620853068470)
XLA Ops:
  0.7 0.9 broadcast_subtract_fusion
  1.5 1.1 convert.9
  2.8 0.7 convert_element_type.66
  3.7 0.8 pad_maximum_fusion.1.tar
  4.6 30.4 %gather.1 = (bf16[448,1024]{1,0:T(8,128)(2,1)}, bf16[1024,1024]{1,0:T(8,128)(2,1)}, bf16[1024,1024]{1,0:T(8,128)(2,1)}, bf16[2,176,1024]{2,1,0:T(8,128)(2,1)}, bf16[2,176,512]{2,1,0:T(8,128)(2,1)}) custom-call(bf16[896,512]{1,0:T(8,128)(2,1)} %tok.1, bf16[1024,512]{1,0:T(8,128)(2,1)} %one.1, bf16[1024,512]{1,0:T(8,128)(2,1)} %two.1, bf16[176,1024]{1,0:T(8,128)(2,1)} %head.1, ...), custom_call_target="tpu_custom_call" | custom-call | tf_op jit(solution)/shard_map/gather/pallas_call | solution.py:145
  35.0 4.4 %multiply_convert_fusion.1 = (bf16[448,1024]{1,0:T(8,128)(2,1)S(1)}, f32[448,1024]{1,0:T(8,128)}) fusion(bf16[448,1024]{1,0:T(8,128)(2,1)} %get-tuple-element.16, bf16[1024,1024]{1,0:T(8,128)(2,1)} %get-tuple-element.17), kind=kOutput, calls=%fused_computation.18 | convolution fusion | flops 941817856 | bytes 5767168 | tf_op jit(solution)/shard_map/dot_general | solution.py:361
  39.4 2.8 %multiply_convert_fusion = (bf16[448,1024]{1,0:T(8,128)(2,1)}, f32[448,1024]{1,0:T(8,128)}) fusion(bf16[448,1024]{1,0:T(8,128)(2,1)S(1)} %get-tuple-element.35, bf16[1024,1024]{1,0:T(8,128)(2,1)S(1)} %copy-done.7), kind=kOutput, calls=%fused_computation.16 | convolution fusion | flops 941817856 | bytes 5767168 | tf_op jit(solution)/shard_map/dot_general | solution.py:361
  43.6 2.2 %multiply_reduce_fusion = (f32[88]{0:T(128)S(1)}, f32[88]{0:T(128)S(1)}, f32[88,4,448]{2,0,1:T(8,128)S(1)}) fusion(f32[4,448]{1,0:T(4,128)S(1)} %get-tuple-element.29, f32[4,448]{1,0:T(4,128)S(1)} %get-tuple-element.30, f32[4,448]{1,0:T(4,128)S(1)} %get-tuple-element.40, pred[88,4]{0,1:T(4,128)(4,1)S(1)} %copy.19, pred[88,4]{0,1:T(4,128)(4,1)S(1)} %copy.18, ...), kind=kOutput, calls=%fused_computation.29 | convolution fusion | flops 324222784 | bytes 2922880 | tf_op jit(solution)/shard_map/dot_general | solution.py:361
  45.8 0.6 select_maximum_fusion.v_ref
  46.4 11.1 %total.1 = f32[8,128]{1,0:T(8,128)} custom-call(f32[8,128]{1,0:T(8,128)} %select_maximum_fusion.v_ref), custom_call_target="tpu_custom_call" | custom-call | tf_op jit(solution)/shard_map/total/pallas_call | solution.py:205
  58.2 0.8 fusion.19
  59.7 1.1 fusion.5
  61.2 0.6 copy-done.11
  61.9 1.7 %fusion.11 = bf16[448,1024]{1,0:T(8,128)(2,1)S(1)} fusion(f32[448,1024]{1,0:T(8,128)S(1)} %copy-done.11, bf16[448,1024]{1,0:T(8,128)(2,1)S(1)} %fusion.5, bf16[1024,1024]{1,0:T(8,128)(2,1)S(1)} %copy-done.8), kind=kOutput, calls=%fused_computation.15 | convolution fusion | flops 944111616 | bytes 5767168 | tf_op jit(solution)/shard_map/dot_general | solution.py:361
  63.7 2.1 %convolution_convert_fusion.2.refs_3_ = bf16[448,1024]{1,0:T(8,128)(2,1)} fusion(bf16[448,1024]{1,0:T(8,128)(2,1)S(1)} %fusion.11, bf16[1024,1024]{1,0:T(8,128)(2,1)S(1)} %copy-done.6), kind=kOutput, calls=%fused_computation.20 | convolution fusion | flops 939982848 | bytes 3932160 | tf_op jit(solution)/shard_map/dot_general | solution.py:361
  66.5 1.3 %copy.23 = bf16[1024,512]{1,0:T(8,128)(2,1)} copy(bf16[1024,512]{0,1:T(8,128)(2,1)S(1)} %pad_maximum_fusion) | data formatting | bytes 2097152 | tf_op jit(solution)/shard_map/concatenate | solution.py:412
  68.1 2.6 %convolution_convert_fusion = bf16[1024,1024]{1,0:T(8,128)(2,1)} fusion(bf16[448,1024]{1,0:T(8,128)(2,1)S(1)} %copy-done.14, bf16[448,1024]{1,0:T(8,128)(2,1)S(1)} %copy-done.16), kind=kOutput, calls=%fused_computation.2 | convolution fusion | flops 940572672 | bytes 3932160 | tf_op jit(solution)/shard_map/dot_general | solution.py:361
  70.7 2.6 %convolution_convert_fusion.1 = bf16[1024,1024]{1,0:T(8,128)(2,1)} fusion(bf16[448,1024]{1,0:T(8,128)(2,1)S(1)} %copy-done.9, bf16[448,1024]{1,0:T(8,128)(2,1)S(1)} %copy-done.18), kind=kOutput, calls=%fused_computation.3 | convolution fusion | flops 940572672 | bytes 3932160 | tf_op jit(solution)/shard_map/dot_general | solution.py:361
  73.4 37.2 %scatter.1 = (f32[64,512]{1,0:T(8,128)}, f32[64,512]{1,0:T(8,128)}, f32[64,256]{1,0:T(8,128)}, bf16[448,512]{1,0:T(8,128)(2,1)}) custom-call(bf16[2,2,2,2,64,1024]{5,4,3,2,1,0:T(8,128)(2,1)} %bitcast.54, bf16[2,2,2,2,64,1024]{5,4,3,2,1,0:T(8,128)(2,1)} %bitcast.53, bf16[2,2,2,2,64,512]{5,4,3,2,1,0:T(8,128)(2,1)} %bitcast.52, ...), custom_call_target="tpu_custom_call" | custom-call | tf_op jit(solution)/shard_map/scatter/pallas_call | solution.py:347
  110.9 2.5 %fusion.12 = f32[896,512]{1,0:T(8,128)} fusion(pred[896]{0:T(1024)(128)(4,1)S(1)} %iota.24, bf16[448,512]{1,0:T(8,128)(2,1)} %get-tuple-element.19, bf16[448,512]{1,0:T(8,128)(2,1)S(1)} %constant_dynamic-slice_fusion), kind=kLoop, calls=%fused_computation.25 | loop fusion | flops 917504 | bytes 2753408 | tf_op jit(solution)/shard_map/convert_element_type | solution.py:423
  113.3 0.6 slice_bitcast_fusion.2
  114.0 0.6 reduce_sum.29
  115.2 0.7 copy.32
  115.9 0.7 copy.33
  (62 shorter events, 4.1 us)
Async XLA Ops:
  35.0 4.5 %copy-start.7 = (bf16[1024,1024]{1,0:T(8,128)(2,1)S(1)}, bf16[1024,1024]{1,0:T(8,128)(2,1)}, u32[]{:S(2)}) copy-start(bf16[1024,1024]{1,0:T(8,128)(2,1)} %get-tuple-element.18) | copy-start | bytes 6291460
  39.4 2.8 %copy-start.13 = (bf16[448,1024]{1,0:T(8,128)(2,1)}, bf16[448,1024]{1,0:T(8,128)(2,1)S(1)}, u32[]{:S(2)}) copy-start(bf16[448,1024]{1,0:T(8,128)(2,1)S(1)} %get-tuple-element.35) | copy-start | bytes 2752516
  39.4 2.8 %copy-start.2 = (bf16[2,176,512]{2,1,0:T(8,128)(2,1)S(1)}, bf16[2,176,512]{2,1,0:T(8,128)(2,1)}, u32[]{:S(2)}) copy-start(bf16[2,176,512]{2,1,0:T(8,128)(2,1)} %get-tuple-element.14) | copy-start | bytes 1081348
  42.3 1.1 copy-start.1
  45.8 13.8 %copy-start.12 = (f32[448,1024]{1,0:T(8,128)S(1)}, f32[448,1024]{1,0:T(8,128)}, u32[]{:S(2)}) copy-start(f32[448,1024]{1,0:T(8,128)} %get-tuple-element.38) | copy-start | bytes 5505028
  59.6 1.6 %copy-start.8 = (bf16[1024,1024]{1,0:T(8,128)(2,1)S(1)}, bf16[1024,1024]{1,0:T(8,128)(2,1)}, u32[]{:S(2)}) copy-start(bf16[1024,1024]{1,0:T(8,128)(2,1)} %get-tuple-element.18) | copy-start | bytes 6291460
  59.6 2.2 %copy-start.11 = (f32[448,1024]{1,0:T(8,128)S(1)}, f32[448,1024]{1,0:T(8,128)}, u32[]{:S(2)}) copy-start(f32[448,1024]{1,0:T(8,128)} %get-tuple-element.36) | copy-start | bytes 5505028
  60.8 2.9 %copy-start.15 = (bf16[448,1024]{1,0:T(8,128)(2,1)}, bf16[448,1024]{1,0:T(8,128)(2,1)S(1)}, u32[]{:S(2)}) copy-start(bf16[448,1024]{1,0:T(8,128)(2,1)S(1)} %fusion.5) | copy-start | bytes 2752516
  61.9 1.8 %copy-start.6 = (bf16[1024,1024]{1,0:T(8,128)(2,1)S(1)}, bf16[1024,1024]{1,0:T(8,128)(2,1)}, u32[]{:S(2)}) copy-start(bf16[1024,1024]{1,0:T(8,128)(2,1)} %get-tuple-element.17) | copy-start | bytes 6291460
  63.6 2.1 %copy-start.17 = (bf16[448,1024]{1,0:T(8,128)(2,1)}, bf16[448,1024]{1,0:T(8,128)(2,1)S(1)}, u32[]{:S(2)}) copy-start(bf16[448,1024]{1,0:T(8,128)(2,1)S(1)} %fusion.11) | copy-start | bytes 2752516
  63.6 2.1 %copy-start.10 = (bf16[448,1024]{1,0:T(8,128)(2,1)S(1)}, bf16[448,1024]{1,0:T(8,128)(2,1)}, u32[]{:S(2)}) copy-start(bf16[448,1024]{1,0:T(8,128)(2,1)} %get-tuple-element.37) | copy-start | bytes 2752516
  66.4 1.4 %copy-start.14 = (bf16[448,1024]{1,0:T(8,128)(2,1)S(1)}, bf16[448,1024]{1,0:T(8,128)(2,1)}, u32[]{:S(2)}) copy-start(bf16[448,1024]{1,0:T(8,128)(2,1)} %copy-done.13) | copy-start | bytes 2752516
  66.4 1.7 %copy-start.16 = (bf16[448,1024]{1,0:T(8,128)(2,1)S(1)}, bf16[448,1024]{1,0:T(8,128)(2,1)}, u32[]{:S(2)}) copy-start(bf16[448,1024]{1,0:T(8,128)(2,1)} %copy-done.15) | copy-start | bytes 2752516
  68.1 2.6 %copy-start.9 = (bf16[448,1024]{1,0:T(8,128)(2,1)S(1)}, bf16[448,1024]{1,0:T(8,128)(2,1)}, u32[]{:S(2)}) copy-start(bf16[448,1024]{1,0:T(8,128)(2,1)} %get-tuple-element.16) | copy-start | bytes 2752516
  68.1 2.6 %copy-start.18 = (bf16[448,1024]{1,0:T(8,128)(2,1)S(1)}, bf16[448,1024]{1,0:T(8,128)(2,1)}, u32[]{:S(2)}) copy-start(bf16[448,1024]{1,0:T(8,128)(2,1)} %copy-done.17) | copy-start | bytes 2752516
  73.4 37.2 %copy-start = (bf16[448,1024]{1,0:T(8,128)(2,1)S(1)}, bf16[448,1024]{1,0:T(8,128)(2,1)}, u32[]{:S(2)}) copy-start(bf16[448,1024]{1,0:T(8,128)(2,1)} %convolution_convert_fusion.2.refs_3_) | copy-start | bytes 2752516
  110.6 2.7 %copy-start.5 = (f32[64,256]{1,0:T(8,128)S(1)}, f32[64,256]{1,0:T(8,128)}, u32[]{:S(2)}) copy-start(f32[64,256]{1,0:T(8,128)} %get-tuple-element.22) | copy-start | bytes 196612
  110.6 4.6 %copy-start.4 = (f32[64,512]{1,0:T(8,128)S(1)}, f32[64,512]{1,0:T(8,128)}, u32[]{:S(2)}) copy-start(f32[64,512]{1,0:T(8,128)} %get-tuple-element.48) | copy-start | bytes 393220
  110.6 5.3 %copy-start.3 = (f32[64,512]{1,0:T(8,128)S(1)}, f32[64,512]{1,0:T(8,128)}, u32[]{:S(2)}) copy-start(f32[64,512]{1,0:T(8,128)} %get-tuple-element.49) | copy-start | bytes 393220

commit v3 on v2

--- a/solution.py
+++ b/solution.py
@@ -13,6 +13,7 @@
 LONP = 224
 MESH = pl.DeviceIdType.MESH
 VMEM = pl.BlockSpec(memory_space=pltpu.VMEM)
+ANY = pl.BlockSpec(memory_space=pl.ANY)
 
 
 def bent(z):
@@ -36,14 +37,14 @@
     pl.semaphore_wait(barrier, len(partners))
 
 
-def params(number):
+def params(number, mib):
     return pltpu.CompilerParams(
-        collective_id=number, has_side_effects=True, vmem_limit_bytes=60 * 2**20
+        collective_id=number, has_side_effects=True, vmem_limit_bytes=mib * 2**20
     )
 
 
 def gather_kernel(
-    tok, one, two, head, tar, o_tok, o_one, o_two, o_head, o_tar, send, recv, local
+    tok, one, two, head, tar, o_tok, o_one, o_two, o_head, o_tar, h_one, h_two, h_head, h_tok, h_tar, send, recv, local
 ):
     s, x = lax.axis_index("space"), lax.axis_index("tensor")
     other = 1 - x
@@ -89,15 +90,20 @@
         remote(tok.at[span(other, half), :], o_tok.at[:, span(x, width)], 24, across),
         remote(tar.at[other], o_tar.at[x], 25, across),
     ]
-    own = [
-        pltpu.make_async_copy(one, o_one.at[:, span(x, width)], local.at[0]),
-        pltpu.make_async_copy(two, o_two.at[:, span(x, width)], local.at[1]),
-        pltpu.make_async_copy(head, o_head.at[x], local.at[2]),
-        pltpu.make_async_copy(tok.at[span(x, half), :], o_tok.at[:, span(x, width)], local.at[3]),
-        pltpu.make_async_copy(tar.at[x], o_tar.at[x], local.at[4]),
+    moves = [
+        (one, h_one, o_one.at[:, span(x, width)]),
+        (two, h_two, o_two.at[:, span(x, width)]),
+        (head, h_head, o_head.at[x]),
+        (tok.at[span(x, half), :], h_tok, o_tok.at[:, span(x, width)]),
+        (tar.at[x], h_tar, o_tar.at[x]),
     ]
-    for copy in own:
+    held = [pltpu.make_async_copy(a, b, local.at[n]) for n, (a, b, _) in enumerate(moves)]
+    own = [pltpu.make_async_copy(b, c, local.at[5 + n]) for n, (_, b, c) in enumerate(moves)]
+    for copy in held:
         copy.start()
+    for first, second in zip(held, own):
+        first.wait()
+        second.start()
 
     def pass_on(k, q, slot, target):
         piece = places[k](other, q)
@@ -151,14 +157,19 @@
             shape((2,) + head.shape, head.dtype),
             shape(targets.shape, targets.dtype),
         ),
-        in_specs=[VMEM] * 5,
-        out_specs=[VMEM] * 5,
+        in_specs=[ANY] * 5,
+        out_specs=[ANY] * 5,
         scratch_shapes=[
+            pltpu.VMEM(first.shape, first.dtype),
+            pltpu.VMEM(second.shape, second.dtype),
+            pltpu.VMEM(head.shape, head.dtype),
+            pltpu.VMEM((half, width), tokens.dtype),
+            pltpu.VMEM(targets.shape[1:], targets.dtype),
             pltpu.SemaphoreType.DMA((26,)),
             pltpu.SemaphoreType.DMA((26,)),
-            pltpu.SemaphoreType.DMA((5,)),
+            pltpu.SemaphoreType.DMA((10,)),
         ],
-        compiler_params=params(0),
+        compiler_params=params(0, 16),
         name="gather",
     )(tokens, first, second, head, targets)
 
@@ -214,7 +225,7 @@
             pltpu.SemaphoreType.DMA((6 + groups,)),
             pltpu.SemaphoreType.DMA((6 + groups,)),
         ],
-        compiler_params=params(1),
+        compiler_params=params(1, 4),
         name="total",
     )(values)
 
@@ -250,7 +261,9 @@
     away = [refs[bits * k : bits * (k + 1)] for k in range(parts)]
     refs = refs[parts * bits :]
     kept = [refs[bits * k : bits * (k + 1)] for k in range(parts)]
-    send, recv = refs[parts * bits :]
+    refs = refs[parts * bits :]
+    near_in = refs[:parts]
+    send, recv, local = refs[parts:]
     s, x = lax.axis_index("space"), lax.axis_index("tensor")
 
     def peer(bit):
@@ -289,6 +302,12 @@
         copy = start(k, 0, ref.at[part(ref, left, order[0], False)])
         left_now = [b for b in left if b != order[0]]
         state.append((ref.at[part(ref, left, order[0], True)], left_now, copy))
+    inner = []
+    for k in range(parts):
+        ref, left, copy = state[k]
+        inner.append(pltpu.make_async_copy(ref, near_in[k], local.at[k]))
+        inner[k].start()
+        state[k] = (near_in[k], left, copy)
     width = tok.shape[1] // 2
     tail = pltpu.make_async_remote_copy(
         src_ref=tok.at[:, pl.ds(pl.multiple_of((1 - x) * width, width), width)],
@@ -309,6 +328,8 @@
             ref, left, copy = state[k]
             arrived = landing[k][n]
             copy.wait_recv()
+            if n == 0:
+                inner[k].wait()
             if n == count - 1:
                 outs[which][pl.ds(first, rows), :] = added(ref, arrived, ...)
                 continue
@@ -342,17 +363,18 @@
     scratch = [pltpu.VMEM(shape, jnp.bfloat16) for found in shapes for shape in found]
     scratch += [pltpu.VMEM(shape, jnp.bfloat16) for found in shapes for shape in found[1:]]
     scratch += [pltpu.VMEM(shape, jnp.float32) for found in shapes for shape in found[1:]]
+    scratch += [pltpu.VMEM(found[0], jnp.bfloat16) for found in shapes]
     slots = len(plan) * (bits + 1) + 1
     outs = [shapes[which][-1][-1] for which in range(3)]
     return pl.pallas_call(
         functools.partial(scatter_kernel, bits, plan),
         out_shape=tuple(jax.ShapeDtypeStruct((rows, width), jnp.float32) for width in outs)
         + (jax.ShapeDtypeStruct((tok.shape[0], tok.shape[1] // 2), tok.dtype),),
-        in_specs=[VMEM] * 4,
-        out_specs=[VMEM] * 4,
+        in_specs=[ANY] * 4,
+        out_specs=[VMEM] * 3 + [ANY],
         scratch_shapes=scratch
-        + [pltpu.SemaphoreType.DMA((slots,)), pltpu.SemaphoreType.DMA((slots,))],
-        compiler_params=params(2),
+        + [pltpu.SemaphoreType.DMA((n,)) for n in (slots, slots, len(plan))],
+        compiler_params=params(2, 28),
         name="scatter",
     )(*grads, tok)
 

time: 118 us -> 106 us (0.90)
  Pallas kernels: 78.7 us -> 69.4 us
  other arithmetic: 8.7 us -> 6.32 us
    pallas_call x1, Pallas kernels: 30.4 us -> 25.8 us  [gather(): pl.pallas_call(gather_kernel, out_shape=(shape((half, 2 * width), tokens....]
    pallas_call x1, Pallas kernels: 37.2 us -> 33.6 us  [scatter(): pl.pallas_call(functools.partial(scatter_kernel, bits, plan), out_shape=t...]
    unnamed x40 -> x34, local copies, waits for them, and re-layouts: 2.76 us -> 2.97 us
where the time goes in v3:
time: 106 us
  Pallas kernels  69.4 us (65%)
  matrix products  20.5 us (19%)
  other arithmetic  6.32 us (6%)
  local copies, waits for them, and re-layouts  6.11 us (6%)
  between operations  3.46 us (3%)
    pallas_call x1, Pallas kernels, scatter(): pl.pallas_call(functools.partial(scatter_kernel, bits, plan), out_shape=t...  33.6 us
    pallas_call x1, Pallas kernels, gather(): pl.pallas_call(gather_kernel, out_shape=(shape((half, 2 * width), tokens....  25.8 us
    dot_general x9, matrix products, mix(): lax.dot_general(a, b, ((dims[:1], dims[1:]), ((), ())), preferred_element...  20.5 us
    pallas_call x1, Pallas kernels, total(): pl.pallas_call(functools.partial(total_kernel, groups), out_shape=jax.Sha...  9.99 us
    unnamed x34, local copies, waits for them, and re-layouts  2.97 us

profile of v3, /device:TPU:0, one launch (start us, length us, event | category | flops | bytes accessed | tf_op | source)
XLA Modules:
  0.0 105.9 jit_solution(15226293181727636495)
XLA Ops:
  0.7 1.6 %broadcast_subtract_fusion = (f32[4,448]{1,0:T(4,128)S(1)}, f32[4,448]{1,0:T(4,128)S(1)}, f32[4,448]{1,0:T(4,128)}) fusion(s32[4,896]{1,0:T(4,128)} %param.13, s32[]{:T(128)S(6)} %select_n.39, s32[4]{0:T(128)S(1)} %and_select_fusion, s32[448]{0:T(512)S(1)} %fusion.17), kind=kLoop, calls=%fused_computation.45 | loop fusion | flops 10752 | bytes 30484 | tf_op jit(solution)/shard_map/sub | solution.py:413
  2.3 1.1 %convert.9 = bf16[176,896]{1,0:T(8,128)(2,1)S(1)} convert(f32[176,896]{1,0:T(8,128)} %param.12) | non-fusion elementwise | flops 157696 | bytes 946176 | tf_op jit(solution)/shard_map/convert.6
  3.5 0.7 convert_element_type.66
  4.6 1.2 %copy-done.2 = bf16[896,512]{1,0:T(8,128)(2,1)S(1)} copy-done((bf16[896,512]{1,0:T(8,128)(2,1)S(1)}, bf16[896,512]{1,0:T(8,128)(2,1)}, u32[]{:S(2)}) %copy-start.2) | copy-done | bytes 917528
  5.8 25.8 %gather.1 = (bf16[448,1024]{1,0:T(8,128)(2,1)S(1)}, bf16[1024,1024]{1,0:T(8,128)(2,1)S(1)}, bf16[1024,1024]{1,0:T(8,128)(2,1)S(1)}, bf16[2,176,1024]{2,1,0:T(8,128)(2,1)S(1)}, bf16[2,176,512]{2,1,0:T(8,128)(2,1)S(1)}) custom-call(bf16[896,512]{1,0:T(8,128)(2,1)S(1)} %copy-done.2, bf16[1024,512]{1,0:T(8,128)(2,1)S(1)} %copy-done, ...), custom_call_target="tpu_custom_call" | custom-call | tf_op jit(solution)/shard_map/gather/pallas_call | solution.py:151
  31.7 2.9 %multiply_convert_fusion.1 = (bf16[448,1024]{1,0:T(8,128)(2,1)S(1)}, f32[448,1024]{1,0:T(8,128)}) fusion(bf16[448,1024]{1,0:T(8,128)(2,1)S(1)} %get-tuple-element.16, bf16[1024,1024]{1,0:T(8,128)(2,1)S(1)} %get-tuple-element.17), kind=kOutput, calls=%fused_computation.18 | convolution fusion | flops 941817856 | bytes 5767168 | tf_op jit(solution)/shard_map/dot_general | solution.py:383
  34.6 2.8 %multiply_convert_fusion = (bf16[448,1024]{1,0:T(8,128)(2,1)}, f32[448,1024]{1,0:T(8,128)}) fusion(bf16[448,1024]{1,0:T(8,128)(2,1)S(1)} %get-tuple-element.35, bf16[1024,1024]{1,0:T(8,128)(2,1)S(1)} %get-tuple-element.18), kind=kOutput, calls=%fused_computation.16 | convolution fusion | flops 941817856 | bytes 5767168 | tf_op jit(solution)/shard_map/dot_general | solution.py:383
  37.4 0.3 compare_reduce_fusion.1
  38.8 2.1 %multiply_reduce_fusion = (f32[88]{0:T(128)S(1)}, f32[88]{0:T(128)S(1)}, f32[88,4,448]{2,0,1:T(8,128)S(1)}) fusion(f32[4,448]{1,0:T(4,128)S(1)} %get-tuple-element.29, f32[4,448]{1,0:T(4,128)S(1)} %get-tuple-element.30, f32[4,448]{1,0:T(4,128)S(1)} %copy-done.10, pred[88,4]{0,1:T(4,128)(4,1)S(1)} %copy.19, pred[88,4]{0,1:T(4,128)(4,1)S(1)} %copy.18, ...), kind=kOutput, calls=%fused_computation.29 | convolution fusion | flops 324222784 | bytes 2922880 | tf_op jit(solution)/shard_map/dot_general | solution.py:383
  41.0 10.0 %total.1 = f32[8,128]{1,0:T(8,128)S(1)} custom-call(f32[8,128]{1,0:T(8,128)S(1)} %select_maximum_fusion.v_ref), custom_call_target="tpu_custom_call" | custom-call | tf_op jit(solution)/shard_map/total/pallas_call | solution.py:216
  52.3 3.8 %fusion.5 = bf16[448,1024]{1,0:T(8,128)(2,1)} fusion(f32[448,1024]{1,0:T(8,128)} %get-tuple-element.38, bf16[352,448]{1,0:T(8,128)(2,1)S(1)} %convert_element_type.74, bf16[352,1024]{1,0:T(8,128)(2,1)S(1)} %bitcast.55), kind=kOutput, calls=%fused_computation.9 | convolution fusion | flops 327548928 | bytes 3788800 | tf_op jit(solution)/shard_map/dot_general | solution.py:383
  56.1 3.1 %fusion.11 = bf16[448,1024]{1,0:T(8,128)(2,1)S(1)} fusion(f32[448,1024]{1,0:T(8,128)S(1)} %copy-done.12, bf16[448,1024]{1,0:T(8,128)(2,1)} %fusion.5, bf16[1024,1024]{1,0:T(8,128)(2,1)S(1)} %copy-done.7), kind=kOutput, calls=%fused_computation.15 | convolution fusion | flops 944111616 | bytes 5767168 | tf_op jit(solution)/shard_map/dot_general | solution.py:383
  59.2 1.2 %convolution_convert_fusion.2.refs_3_ = bf16[448,1024]{1,0:T(8,128)(2,1)S(1)} fusion(bf16[448,1024]{1,0:T(8,128)(2,1)S(1)} %fusion.11, bf16[1024,1024]{1,0:T(8,128)(2,1)S(1)} %copy-done.5), kind=kOutput, calls=%fused_computation.20 | convolution fusion | flops 939982848 | bytes 3932160 | tf_op jit(solution)/shard_map/dot_general | solution.py:383
  60.4 0.3 copy-done.11
  60.7 0.5 convolution_convert_fusion.3
  61.4 0.5 copy.23
  62.0 2.9 %convolution_convert_fusion = bf16[1024,1024]{1,0:T(8,128)(2,1)S(1)} fusion(bf16[448,1024]{1,0:T(8,128)(2,1)} %copy-done.13, bf16[448,1024]{1,0:T(8,128)(2,1)} %fusion.5), kind=kOutput, calls=%fused_computation.2 | convolution fusion | flops 940572672 | bytes 3932160 | tf_op jit(solution)/shard_map/dot_general | solution.py:383
  64.9 1.3 %convolution_convert_fusion.1 = bf16[1024,1024]{1,0:T(8,128)(2,1)S(1)} fusion(bf16[448,1024]{1,0:T(8,128)(2,1)S(1)} %copy-done.9, bf16[448,1024]{1,0:T(8,128)(2,1)S(1)} %copy-done.15), kind=kOutput, calls=%fused_computation.3 | convolution fusion | flops 940572672 | bytes 3932160 | tf_op jit(solution)/shard_map/dot_general | solution.py:383
  66.2 33.6 %scatter.1 = (f32[64,512]{1,0:T(8,128)S(1)}, f32[64,512]{1,0:T(8,128)S(1)}, f32[64,256]{1,0:T(8,128)S(1)}, bf16[448,512]{1,0:T(8,128)(2,1)S(1)}) custom-call(bf16[2,2,2,2,64,1024]{5,4,3,2,1,0:T(8,128)(2,1)S(1)} %bitcast.54, bf16[2,2,2,2,64,1024]{5,4,3,2,1,0:T(8,128)(2,1)S(1)} %bitcast.53, bf16[2,2,2,2,64,512]{5,4,3,2,1,0:T(8,128)(2,1)S(1)} %bitcast.52, ...), custom_call_target="tpu_custom_call" | custom-call | tf_op jit(solution)/shard_map/scatter/pallas_call | solution.py:369
  100.1 1.4 %fusion.12 = f32[896,512]{1,0:T(8,128)} fusion(pred[896]{0:T(1024)(128)(4,1)S(1)} %iota.24, bf16[448,512]{1,0:T(8,128)(2,1)S(1)} %get-tuple-element.19, bf16[448,512]{1,0:T(8,128)(2,1)S(1)} %constant_dynamic-slice_fusion), kind=kLoop, calls=%fused_computation.25 | loop fusion | flops 917504 | bytes 2753408 | tf_op jit(solution)/shard_map/convert_element_type | solution.py:445
  101.5 0.6 slice_bitcast_fusion.2
  102.2 0.6 reduce_sum.29
  103.4 0.7 copy.32
  104.1 0.7 copy.33
  (56 shorter events, 2.7 us)
Async XLA Ops:
  0.6 4.0 %copy-start.1 = (bf16[1024,512]{1,0:T(8,128)(2,1)S(1)}, bf16[1024,512]{1,0:T(8,128)(2,1)}, u32[]{:S(2)}) copy-start(bf16[1024,512]{1,0:T(8,128)(2,1)} %two.1) | copy-start | bytes 3145732
  0.6 4.0 %copy-start.3 = (bf16[176,1024]{1,0:T(8,128)(2,1)S(1)}, bf16[176,1024]{1,0:T(8,128)(2,1)}, u32[]{:S(2)}) copy-start(bf16[176,1024]{1,0:T(8,128)(2,1)} %head.1) | copy-start | bytes 1081348
  0.7 4.0 %copy-start = (bf16[1024,512]{1,0:T(8,128)(2,1)S(1)}, bf16[1024,512]{1,0:T(8,128)(2,1)}, u32[]{:S(2)}) copy-start(bf16[1024,512]{1,0:T(8,128)(2,1)} %one.1) | copy-start | bytes 3145732
  4.6 1.2 %copy-start.2 = (bf16[896,512]{1,0:T(8,128)(2,1)S(1)}, bf16[896,512]{1,0:T(8,128)(2,1)}, u32[]{:S(2)}) copy-start(bf16[896,512]{1,0:T(8,128)(2,1)} %tok.1) | copy-start | bytes 2752516
  31.6 2.9 %copy-start.4 = (bf16[1024,1024]{1,0:T(8,128)(2,1)}, bf16[1024,1024]{1,0:T(8,128)(2,1)S(1)}, u32[]{:S(2)}) copy-start(bf16[1024,1024]{1,0:T(8,128)(2,1)S(1)} %get-tuple-element.17) | copy-start | bytes 6291460
  31.7 2.9 %copy-start.8 = (bf16[448,1024]{1,0:T(8,128)(2,1)}, bf16[448,1024]{1,0:T(8,128)(2,1)S(1)}, u32[]{:S(2)}) copy-start(bf16[448,1024]{1,0:T(8,128)(2,1)S(1)} %get-tuple-element.16) | copy-start | bytes 2752516
  31.7 2.9 %copy-start.6 = (bf16[1024,1024]{1,0:T(8,128)(2,1)}, bf16[1024,1024]{1,0:T(8,128)(2,1)S(1)}, u32[]{:S(2)}) copy-start(bf16[1024,1024]{1,0:T(8,128)(2,1)S(1)} %get-tuple-element.18) | copy-start | bytes 6291460
  34.6 3.1 %copy-start.13 = (bf16[448,1024]{1,0:T(8,128)(2,1)}, bf16[448,1024]{1,0:T(8,128)(2,1)S(1)}, u32[]{:S(2)}) copy-start(bf16[448,1024]{1,0:T(8,128)(2,1)S(1)} %get-tuple-element.35) | copy-start | bytes 2752516
  38.1 0.7 copy-start.10
  52.3 3.8 %copy-start.7 = (bf16[1024,1024]{1,0:T(8,128)(2,1)S(1)}, bf16[1024,1024]{1,0:T(8,128)(2,1)}, u32[]{:S(2)}) copy-start(bf16[1024,1024]{1,0:T(8,128)(2,1)} %copy-done.6) | copy-start | bytes 6291460
  52.3 3.8 %copy-start.12 = (f32[448,1024]{1,0:T(8,128)S(1)}, f32[448,1024]{1,0:T(8,128)}, u32[]{:S(2)}) copy-start(f32[448,1024]{1,0:T(8,128)} %get-tuple-element.36) | copy-start | bytes 5505028
  56.1 3.1 %copy-start.5 = (bf16[1024,1024]{1,0:T(8,128)(2,1)S(1)}, bf16[1024,1024]{1,0:T(8,128)(2,1)}, u32[]{:S(2)}) copy-start(bf16[1024,1024]{1,0:T(8,128)(2,1)} %copy-done.4) | copy-start | bytes 6291460
  59.2 1.2 %copy-start.14 = (bf16[448,1024]{1,0:T(8,128)(2,1)}, bf16[448,1024]{1,0:T(8,128)(2,1)S(1)}, u32[]{:S(2)}) copy-start(bf16[448,1024]{1,0:T(8,128)(2,1)S(1)} %fusion.11) | copy-start | bytes 2752516
  59.2 1.5 %copy-start.11 = (bf16[448,1024]{1,0:T(8,128)(2,1)S(1)}, bf16[448,1024]{1,0:T(8,128)(2,1)}, u32[]{:S(2)}) copy-start(bf16[448,1024]{1,0:T(8,128)(2,1)} %get-tuple-element.37) | copy-start | bytes 2752516
  62.0 2.9 %copy-start.9 = (bf16[448,1024]{1,0:T(8,128)(2,1)S(1)}, bf16[448,1024]{1,0:T(8,128)(2,1)}, u32[]{:S(2)}) copy-start(bf16[448,1024]{1,0:T(8,128)(2,1)} %copy-done.8) | copy-start | bytes 2752516
  62.0 2.9 %copy-start.15 = (bf16[448,1024]{1,0:T(8,128)(2,1)S(1)}, bf16[448,1024]{1,0:T(8,128)(2,1)}, u32[]{:S(2)}) copy-start(bf16[448,1024]{1,0:T(8,128)(2,1)} %copy-done.14) | copy-start | bytes 2752516
